TPU v7x, 256 devices: a whole 4x4x8 slice. The times are simulated.
256 devices in a mesh: gz: 32 (over x, z), gy: 8 (over y, core).
Axes of the slice: x: 4, y: 4, z: 8, core: 2. Of those that a mesh axis runs over, the one named last changes fastest.
Arguments:
- fields: float32 [2, 256, 256, 128], P(None, 'gz', 'gy'), may hold values from -7 to 8
- residual: float32 [2, 256, 256, 128], P(None, 'gz', 'gy'), may hold values from -14 to 14
- past_fields: float32 [20, 2, 256, 256, 128], P(None, None, 'gz', 'gy'), may hold values from -7 to 8
- past_residuals: float32 [20, 2, 256, 256, 128], P(None, None, 'gz', 'gy'), may hold values from -14 to 14
Outputs:
- new_fields: float32 [2, 256, 256, 128], P(None, 'gz', 'gy')
- summary: float32 [3], replicated
All inputs are finite; a program needn't handle non-finite values.
Results may differ from a plain program's by a relative error of at most 0.0003.
Values sent between devices are 32-bit elements; how exact they have to be, the bound alone decides.
No kernel may reach another device: no remote copies, remote signals or barrier semaphores. Data moves between devices by JAX's collectives and lax.ppermute only.
A program may use at most 64 MiB of HBM per device.

v0:
```python
import functools
import math

import jax
import jax.numpy as jnp
from jax import lax
from jax.sharding import Mesh
from jax.sharding import PartitionSpec as P

GZ = ("gz_0", "gz_1")
GY = ("gy_0", "gy_1")
GZ_GY = ("gz_0", "gz_1", "gy_0", "gy_1")


CHI_N = 20.0
RIDGE = 0.01
STEP_LOCAL = 0.1
EXACT = lax.Precision.HIGHEST


def by_axis(shard, axes):
    return functools.reduce(lax.psum, axes, shard)


def joined_along(tiles, dim):
    tiles = jnp.moveaxis(tiles, 0, dim)
    shape = tiles.shape
    return tiles.reshape(*shape[:dim], shape[dim] * shape[dim + 1], *shape[dim + 2 :])


def copy_for_each(shard, axis):
    count = lax.axis_size(axis)
    return lax.all_to_all(
        jnp.broadcast_to(shard[None], (count, *shard.shape)), axis, 0, 0, tiled=True
    )


def gathered_copies(shard, axis, dim):
    return joined_along(copy_for_each(shard, axis), dim)


def merged_by_axis(shard, axes, combine):
    for axis in axes:
        pieces = jax.tree.map(lambda part: lax.all_gather(part, axis), shard)
        shard = jax.tree.map(lambda part: part[0], pieces)
        for k in range(1, lax.axis_size(axis)):
            shard = combine(shard, jax.tree.map(lambda part: part[k], pieces))
    return shard


def kernel_total(length):
    decay_len = length / 4.0
    offsets = lax.iota(jnp.int32, length).astype(jnp.float32)
    return jnp.sum(jnp.cosh((0.5 * length - offsets) / decay_len))


def kernel_rows(row_first, row_count, col_first, col_count, length):
    decay_len = length / 4.0
    row_index = row_first + lax.iota(jnp.int32, row_count)[:, None]
    col_index = col_first + lax.iota(jnp.int32, col_count)[None, :]
    lag = jnp.mod(row_index - col_index, length).astype(jnp.float32)
    return jnp.cosh((0.5 * length - lag) / decay_len) / kernel_total(length)


def end_moments(first, count, length):
    decay_len = length / 4.0
    place = (first + lax.iota(jnp.int32, count)).astype(jnp.float32) / decay_len
    return jnp.stack([jnp.exp(place), jnp.exp(-place)])


def far_weights(first, count, own_block, blocks, length):
    decay_len = length / 4.0
    place = (first + lax.iota(jnp.int32, count)).astype(jnp.float32) / decay_len
    block_index = lax.iota(jnp.int32, blocks)
    below = block_index < own_block
    above = block_index > own_block
    wide = math.exp(0.5 * length / decay_len)
    rising = jnp.where(below, wide, jnp.where(above, 1.0 / wide, 0.0))
    falling = jnp.where(below, 1.0 / wide, jnp.where(above, wide, 0.0))
    factor = 0.5 / kernel_total(length)
    weight_rising = factor * jnp.exp(-place)[:, None] * rising[None, :]
    weight_falling = factor * jnp.exp(place)[:, None] * falling[None, :]
    return jnp.stack([weight_rising, weight_falling], axis=2).reshape(count, 2 * blocks)


def combine(left_part, right_part):
    return (left_part[0] + right_part[0], jnp.maximum(left_part[1], right_part[1]))


def shards(fields, residual, past_fields, past_residuals):
    history = past_residuals.shape[0]
    species, height_cells, width_cells, line_cells = residual.shape
    height_total = height_cells * lax.axis_size(GZ)
    width_total = width_cells * lax.axis_size(GY)
    cell_total = height_total * width_total * line_cells
    flat_residual = residual.reshape(-1)
    past_rows = past_residuals.reshape(history, -1)
    deltas = flat_residual[None, :] - past_rows
    gram_local = jnp.dot(deltas, deltas.T, precision=EXACT, preferred_element_type=jnp.float32)
    intersect_local = jnp.dot(
        deltas, flat_residual, precision=EXACT, preferred_element_type=jnp.float32
    )
    residual_square = jnp.sum(residual * residual)
    field_square = jnp.sum(fields * fields)
    gram_matrix, intersect, residual_total, field_total = (
        by_axis(gram_local, GZ_GY),
        by_axis(intersect_local, GZ_GY),
        by_axis(residual_square, GZ_GY),
        by_axis(field_square, GZ_GY),
    )
    diagonal_shift = RIDGE * jnp.trace(gram_matrix) / history + 1.0
    system = gram_matrix + diagonal_shift * jnp.eye(history, dtype=jnp.float32)
    factor = jnp.linalg.cholesky(system)
    forward = lax.linalg.triangular_solve(factor, intersect[:, None], left_side=True, lower=True)
    coeffs = lax.linalg.triangular_solve(
        factor, forward, left_side=True, lower=True, transpose_a=True
    )[:, 0]
    remain_weight = 1.0 - jnp.sum(coeffs)
    field_mixed = remain_weight * fields + jnp.dot(
        coeffs,
        past_fields.reshape(history, -1),
        precision=EXACT,
        preferred_element_type=jnp.float32,
    ).reshape(fields.shape)
    residual_mixed = remain_weight * residual + jnp.dot(
        coeffs, past_rows, precision=EXACT, preferred_element_type=jnp.float32
    ).reshape(residual.shape)
    width_first = lax.axis_index(GY) * width_cells
    kernel = kernel_rows(0, height_total, 0, height_total, height_total)
    smooth = jnp.einsum(
        "ab,sbyx->sayx",
        kernel,
        lax.all_to_all(residual_mixed, GZ, split_axis=2, concat_axis=1, tiled=True),
        precision=EXACT,
    )
    smoothed_half = lax.all_to_all(smooth, GZ, split_axis=1, concat_axis=2, tiled=True)
    moments = jnp.einsum(
        "ab,szbx->szax",
        end_moments(width_first, width_cells, width_total),
        smoothed_half,
        precision=EXACT,
    )
    every_end = gathered_copies(moments, GY, 2)
    near = jnp.einsum(
        "ab,szbx->szax",
        kernel_rows(width_first, width_cells, width_first, width_cells, width_total),
        smoothed_half,
        precision=EXACT,
    )
    far = jnp.einsum(
        "ab,szbx->szax",
        far_weights(width_first, width_cells, lax.axis_index(GY), lax.axis_size(GY), width_total),
        every_end,
        precision=EXACT,
    )
    smoothed = near + far
    new_fields = field_mixed + STEP_LOCAL * residual_mixed + smoothed
    split_field = new_fields[0] - new_fields[1]
    sum_field = new_fields[0] + new_fields[1]
    energy_local = jnp.sum(split_field * split_field / (4.0 * CHI_N) - 0.5 * sum_field)
    peak_local = jnp.max(jnp.abs(residual_mixed))
    energy_total, largest = merged_by_axis((energy_local, peak_local), GZ_GY, combine)
    relative = jnp.sqrt(residual_total / (field_total + 1.0))
    summary = jnp.stack([energy_total / cell_total, relative, largest])
    return (new_fields, summary)


def solution(mesh):
    torus = Mesh(mesh.devices.reshape(4, 8, 4, 2), ("gz_0", "gz_1", "gy_0", "gy_1"))
    placed = (
        P(None, GZ, GY, None),
        P(None, GZ, GY, None),
        P(None, None, GZ, GY, None),
        P(None, None, GZ, GY, None),
    )
    return jax.shard_map(
        shards, mesh=torus, in_specs=placed, out_specs=(P(None, GZ, GY, None), P()), check_vma=False
    )
```

profile of v0, /device:TPU:1, one launch (start us, length us, event | category | flops | bytes accessed | tf_op | source)
XLA Modules:
  0.0 209.0 jit_solution(14556699594364804850)
XLA Ops:
  0.6 3.2 %broadcast_subtract_fusion = f32[20,2,8,32,128]{4,3,2,1,0:T(8,128)S(1)} fusion(f32[20,2,8,32,128]{4,3,2,1,0:T(8,128)} %param.7, f32[2,8,32,128]{3,2,1,0:T(8,128)} %param.5), kind=kLoop, calls=%fused_computation.8 | loop fusion | flops 1310720 | bytes 10747904 | tf_op jit(solution)/shard_map/sub | solution.py:98
  3.8 8.4 %fusion.10 = f32[20,20]{1,0:T(8,128)S(1)} fusion(f32[20,2,8,32,128]{4,3,2,1,0:T(8,128)S(1)} %broadcast_subtract_fusion), kind=kOutput, calls=%fused_computation.15 | convolution fusion | flops 314572800 | bytes 5244480 | tf_op jit(solution)/shard_map/dot_general | solution.py:99
  12.2 8.1 %fusion.13 = f32[20]{0:T(128)S(1)} fusion(f32[2,8,32,128,1]{3,4,2,1,0:T(1,128)S(1)} %bitcast.136, f32[20,2,8,32,128]{4,3,2,1,0:T(8,128)S(1)} %broadcast_subtract_fusion), kind=kOutput, calls=%fused_computation.17 | convolution fusion | flops 15728640 | bytes 5505104 | tf_op jit(solution)/shard_map/dot_general | solution.py:100
  20.3 14.2 %all-reduce.13 = (f32[20,20]{1,0:T(8,128)S(1)}, f32[20]{0:T(128)S(1)}) all-reduce(f32[20,20]{1,0:T(8,128)S(1)} %fusion.10, f32[20]{0:T(128)S(1)} %fusion.13), channel_id=1, replica_groups=mesh['gz_0'=4,'gz_1'=8,'gy_0'=4,'gy_1'=2] {'gz_0'}, use_global_device_ids=true, to_apply=%region_0.0 | all-reduce | flops 420 | bytes 3360 | tf_op jit(solution)/shard_map/psum | solution.py:22
  34.5 25.3 %all-reduce.9 = (f32[20,20]{1,0:T(8,128)S(1)}, f32[20]{0:T(128)S(1)}) all-reduce(f32[20,20]{1,0:T(8,128)S(1)} %get-tuple-element.18, f32[20]{0:T(128)S(1)} %get-tuple-element.19), channel_id=1, replica_groups=mesh['gz_0'=4,'gz_1'=8,'gy_0'=4,'gy_1'=2] {'gz_1'}, use_global_device_ids=true, to_apply=%region_1.0 | all-reduce | flops 420 | bytes 3360 | tf_op jit(solution)/shard_map/psum | solution.py:22
  59.8 13.4 %all-reduce.11 = (f32[20,20]{1,0:T(8,128)S(1)}, f32[20]{0:T(128)S(1)}) all-reduce(f32[20,20]{1,0:T(8,128)S(1)} %get-tuple-element.6, f32[20]{0:T(128)S(1)} %get-tuple-element.7), channel_id=1, replica_groups=mesh['gz_0'=4,'gz_1'=8,'gy_0'=4,'gy_1'=2] {'gy_0'}, use_global_device_ids=true, to_apply=%region_2.0 | all-reduce | flops 420 | bytes 3360 | tf_op jit(solution)/shard_map/psum | solution.py:22
  73.2 18.5 %all-reduce.15 = (f32[20,20]{1,0:T(8,128)S(1)}, f32[20]{0:T(128)S(1)}) all-reduce(f32[20,20]{1,0:T(8,128)S(1)} %get-tuple-element.12, f32[20]{0:T(128)S(1)} %get-tuple-element.13), channel_id=1, replica_groups=mesh['gz_0'=4,'gz_1'=8,'gy_0'=4,'gy_1'=2] {'gy_1'}, use_global_device_ids=true, to_apply=%region_3.0 | all-reduce | flops 420 | bytes 3360 | tf_op jit(solution)/shard_map/psum | solution.py:22
  93.1 1.8 cholesky.17
  96.3 1.5 custom-call.8
  99.4 9.1 %fusion.4 = f32[1,2,8,32,128]{4,0,3,2,1:T(1,128)S(1)} fusion(f32[2,8,32,128,20]{3,2,1,0,4:T(8,128)} %bitcast.132, f32[1,20]{1,0:T(1,128)S(1)} %get-tuple-element.34), kind=kOutput, calls=%fused_computation.4 | convolution fusion | flops 15728640 | bytes 5505104 | tf_op jit(solution)/shard_map/dot_general | solution.py:125
  110.1 4.0 %all-to-all-start = ((f32[2,8,32,128]{3,1,0,2:T(8,128)}), f32[2,8,32,128]{3,1,0,2:T(8,128)S(1)}, u32[]{:S(2)}, u32[]{:S(2)}) async-start(f32[2,8,32,128]{3,1,0,2:T(8,128)} %copy.21), calls=%async_computation | async-start | bytes 524288 | tf_op jit(solution)/shard_map/all_to_all | solution.py:133
  115.5 8.7 %all-to-all-done = f32[2,8,32,128]{3,1,0,2:T(8,128)S(1)} async-done(((f32[2,8,32,128]{3,1,0,2:T(8,128)}), f32[2,8,32,128]{3,1,0,2:T(8,128)S(1)}, u32[]{:S(2)}, u32[]{:S(2)}) %all-to-all-start) | async-done | bytes 262176 | tf_op jit(solution)/shard_map/all_to_all | solution.py:133
  124.2 1.3 convolution_bitcast_fusion
  126.4 6.8 %all-to-all-start.1 = ((f32[2,256,1,128]{3,0,2,1:T(2,128)}), f32[2,256,1,128]{3,0,2,1:T(2,128)S(1)}, u32[]{:S(2)}, u32[]{:S(2)}) async-start(f32[2,256,1,128]{3,0,2,1:T(2,128)} %copy.24), calls=%async_computation.1 | async-start | bytes 524288 | tf_op jit(solution)/shard_map/all_to_all | solution.py:136
  133.2 9.1 %fusion.6 = f32[1,2,8,32,128]{4,0,3,2,1:T(1,128)S(1)} fusion(f32[2,8,32,128,20]{3,2,1,0,4:T(8,128)} %bitcast.133, f32[1,20]{1,0:T(1,128)S(1)} %get-tuple-element.34), kind=kOutput, calls=%fused_computation.6 | convolution fusion | flops 15728640 | bytes 5505104 | tf_op jit(solution)/shard_map/dot_general | solution.py:119
  143.6 6.9 %all-to-all-start.2 = ((f32[8,2,8,2,128]{4,3,2,1,0:T(2,128)}), f32[8,2,8,2,128]{4,3,2,1,0:T(2,128)S(1)}, u32[]{:S(2)}, u32[]{:S(2)}) async-start(f32[8,2,8,2,128]{4,3,2,1,0:T(2,128)} %broadcast_in_dim.37), calls=%async_computation.2 | async-start | bytes 262144 | tf_op jit(solution)/shard_map/all_to_all | solution.py:33
  153.1 1.3 dynamic-update-slice.7
  154.4 1.4 all-to-all-done.2
  156.2 1.1 fusion.9
  158.0 1.3 dynamic-update-slice.3
  159.3 7.5 %all-reduce.12 = (f32[4]{0:T(128)S(1)}, f32[]{:T(128)}, f32[]{:T(128)}, f32[4]{0:T(128)S(1)}) all-reduce(f32[4]{0:T(128)S(1)} %dynamic-update-slice.7, f32[]{:T(128)} %get-tuple-element.28, f32[]{:T(128)} %get-tuple-element.41, f32[4]{0:T(128)S(1)} %dynamic-update-slice.3), channel_id=1, replica_groups=mesh['gz_0'=4,'gz_1'=8,'gy_0'=4,'gy_1'=2] {'gz_0'}, use_global_device_ids=true, to_apply=%add.4 | all-reduce | flops 10 | bytes 80
  168.3 12.8 %all-reduce.8 = (f32[8]{0:T(128)S(1)}, f32[]{:T(128)}, f32[]{:T(128)}, f32[8]{0:T(128)S(1)}) all-reduce(f32[8]{0:T(128)S(1)} %maximum_dynamic-update-slice_fusion.2, f32[]{:T(128)} %get-tuple-element.15, f32[]{:T(128)} %get-tuple-element.16, ...), channel_id=1, replica_groups=mesh['gz_0'=4,'gz_1'=8,'gy_0'=4,'gy_1'=2] {'gz_1'}, use_global_device_ids=true, to_apply=%add.5 | all-reduce | flops 18 | bytes 144
  182.7 7.8 %all-reduce.10 = (f32[4]{0:T(128)S(1)}, f32[]{:T(128)}, f32[]{:T(128)}, f32[4]{0:T(128)S(1)}) all-reduce(f32[4]{0:T(128)S(1)} %maximum_dynamic-update-slice_fusion, f32[]{:T(128)} %get-tuple-element.3, f32[]{:T(128)} %get-tuple-element.4, f32[4]{0:T(128)S(1)} %add_dynamic-update-slice_fusion), channel_id=1, replica_groups=mesh['gz_0'=4,'gz_1'=8,'gy_0'=4,'gy_1'=2] {'gy_0'}, use_global_device_ids=true, to_apply=%add.6 | all-reduce | flops 10 | bytes 80
  192.2 11.1 %all-reduce.14 = (f32[2]{0:T(128)S(1)}, f32[]{:T(128)}, f32[]{:T(128)}, f32[2]{0:T(128)S(1)}) all-reduce(f32[2]{0:T(128)S(1)} %maximum_dynamic-update-slice_fusion.1, f32[]{:T(128)} %get-tuple-element.9, f32[]{:T(128)} %get-tuple-element.10, ...), channel_id=1, replica_groups=mesh['gz_0'=4,'gz_1'=8,'gy_0'=4,'gy_1'=2] {'gy_1'}, use_global_device_ids=true, to_apply=%add.7 | all-reduce | flops 6 | bytes 48
  (59 shorter events, 17.6 us)
Async XLA Ops:
  3.8 8.4 %copy-start = (f32[2,8,32,128]{3,2,1,0:T(8,128)S(1)}, f32[2,8,32,128]{3,2,1,0:T(8,128)}, u32[]{:S(2)}) copy-start(f32[2,8,32,128]{3,2,1,0:T(8,128)} %param.5) | copy-start | bytes 786436
  12.2 96.3 %copy-start.2 = (f32[2,8,32,128]{3,2,1,0:T(8,128)S(1)}, f32[2,8,32,128]{3,2,1,0:T(8,128)}, u32[]{:S(2)}) copy-start(f32[2,8,32,128]{3,2,1,0:T(8,128)} %param.4) | copy-start | bytes 786436
  110.1 14.1 %all-to-all-start = ((f32[2,8,32,128]{3,1,0,2:T(8,128)}), f32[2,8,32,128]{3,1,0,2:T(8,128)S(1)}, u32[]{:S(2)}, u32[]{:S(2)}) async-start(f32[2,8,32,128]{3,1,0,2:T(8,128)} %copy.21), calls=%async_computation | async-start | bytes 524288 | tf_op jit(solution)/shard_map/all_to_all | solution.py:133
  115.5 35.1 %copy-start.6 = (u32[256]{0:T(256)S(1)}, u32[256]{0:T(256)}, u32[]{:S(2)}) copy-start(u32[256]{0:T(256)} %constant.133) | copy-start | bytes 3076
  115.5 35.7 %copy-start.5 = (u32[256]{0:T(256)S(1)}, u32[256]{0:T(256)}, u32[]{:S(2)}) copy-start(u32[256]{0:T(256)} %constant.138) | copy-start | bytes 3076
  115.5 36.3 %copy-start.4 = (u32[256]{0:T(256)S(1)}, u32[256]{0:T(256)}, u32[]{:S(2)}) copy-start(u32[256]{0:T(256)} %constant.143) | copy-start | bytes 3076
  115.5 37.0 %copy-start.3 = (u32[256]{0:T(256)S(1)}, u32[256]{0:T(256)}, u32[]{:S(2)}) copy-start(u32[256]{0:T(256)} %constant.148) | copy-start | bytes 3076
  126.4 16.2 %all-to-all-start.1 = ((f32[2,256,1,128]{3,0,2,1:T(2,128)}), f32[2,256,1,128]{3,0,2,1:T(2,128)S(1)}, u32[]{:S(2)}, u32[]{:S(2)}) async-start(f32[2,256,1,128]{3,0,2,1:T(2,128)} %copy.24), calls=%async_computation.1 | async-start | bytes 524288 | tf_op jit(solution)/shard_map/all_to_all | solution.py:136
  143.6 12.2 %all-to-all-start.2 = ((f32[8,2,8,2,128]{4,3,2,1,0:T(2,128)}), f32[8,2,8,2,128]{4,3,2,1,0:T(2,128)S(1)}, u32[]{:S(2)}, u32[]{:S(2)}) async-start(f32[8,2,8,2,128]{4,3,2,1,0:T(2,128)} %broadcast_in_dim.37), calls=%async_computation.2 | async-start | bytes 262144 | tf_op jit(solution)/shard_map/all_to_all | solution.py:33
  157.3 51.7 %copy-start.1 = (f32[2,8,32,128]{3,2,1,0:T(8,128)}, f32[2,8,32,128]{3,2,1,0:T(8,128)S(1)}, u32[]{:S(2)}) copy-start(f32[2,8,32,128]{3,2,1,0:T(8,128)S(1)} %fusion.9) | copy-start | bytes 786436
where the time goes:
time: 210 us; the launch traced here: 209 us
  blocking collectives  111 us (53%)
  matrix products  38.7 us (18%)
  starting transfers between devices  17.7 us (8%)
  other arithmetic  16.1 us (8%)
  waiting for transfers between devices  10.3 us (5%)
  local copies, waits for them, and re-layouts  8.82 us (4%)
  between operations  6.67 us (3%)
    psum x4, blocking collectives, by_axis(): return functools.reduce(lax.psum, axes, shard)  71.4 us
    unnamed x4, blocking collectives  39.2 us
    dot_general x1, matrix products, shards(): jnp.dot(coeffs, past_rows, precision=EXACT, preferred_element_type=jnp.fl...  9.13 us
    dot_general x1, matrix products, shards(): jnp.dot(coeffs, past_fields.reshape(history, -1), precision=EXACT, prefer...  9.12 us
    all_to_all x1, waiting for transfers between devices, shards(): lax.all_to_all(residual_mixed, GZ, split_axis=2, concat_axis=1, tiled=True)  8.7 us
    dot_general x1, matrix products, shards(): jnp.dot(deltas, deltas.T, precision=EXACT, preferred_element_type=jnp.flo...  8.36 us
    dot_general x1, matrix products, shards(): jnp.dot(deltas, flat_residual, precision=EXACT, preferred_element_type=jn...  8.13 us
    all_to_all x1, starting transfers between devices, copy_for_each(): lax.all_to_all(jnp.broadcast_to(shard[None], (count, *shard.shape)), axis...  6.93 us
  transfers between devices with their start and end apart: 3, of which 3 were waited for; matrix products, arithmetic and copies ran while one was open for 7% of the time, Pallas kernels for 0%

commit v1 on v0

v1 whole, which is shorter than its diff:
```python
import functools
import math

import jax
import jax.numpy as jnp
from jax import lax
from jax.experimental import pallas as pl
from jax.experimental.pallas import tpu as pltpu
from jax.sharding import PartitionSpec as P

CHI_N = 20.0
RIDGE = 0.01
STEP_LOCAL = 0.1
EXACT = lax.Precision.HIGHEST
HIST = 20
BANDS = HIST + 2
LINES = 512
CHUNK = 64
LANES = 128
PLANES = 8
ROWS = 32
F32 = jnp.float32
BF16 = jnp.bfloat16
LENGTH = 256
DECAY = LENGTH / 4.0
TOTAL = sum(math.cosh((0.5 * LENGTH - d) / DECAY) for d in range(LENGTH))
WIDE = math.exp(0.5 * LENGTH / DECAY)
CELLS = 256 * 256 * 128

VMEM = pl.BlockSpec(memory_space=pltpu.VMEM)


def params(mib, **more):
    return pltpu.CompilerParams(vmem_limit_bytes=mib * 1024 * 1024, **more)


def halves(x):
    high = x.astype(BF16)
    return high, (x - high.astype(F32)).astype(BF16)


def product(a, b, contract):
    return lax.dot_general(a, b, (contract, ((), ())), preferred_element_type=F32)


def split_product(a, b, contract):
    a_high, a_low = halves(a)
    b_high, b_low = halves(b)
    return (
        product(a_high, b_high, contract)
        + product(a_high, b_low, contract)
        + product(a_low, b_high, contract)
    )


def iota(shape, dim):
    return lax.broadcasted_iota(jnp.int32, shape, dim)


def ramp(shape, dim, sign):
    return jnp.exp(iota(shape, dim).astype(F32) * (sign / DECAY))


def near_matrix(count):
    lag = jnp.abs(iota((count, count), 0) - iota((count, count), 1)).astype(F32)
    half = (0.5 * LENGTH - lag) / DECAY
    return (jnp.exp(half) + jnp.exp(-half)) * (0.5 / TOTAL)


def near_value(lag):
    return math.cosh((0.5 * LENGTH - lag) / DECAY) / TOTAL


def far_weight(row, col, width):
    gap = (row - col).astype(F32) * (width / DECAY)
    below = jnp.exp(-gap) * (WIDE * 0.5 / TOTAL)
    above = jnp.exp(-gap) * (0.5 / (WIDE * TOTAL))
    return jnp.where(col < row, below, jnp.where(col > row, above, 0.0))


def gram_kernel(res_ref, fld_ref, past_ref, out_ref, acc_ref):
    step = pl.program_id(0)
    pieces = []
    for k in range(CHUNK // 8):
        rows = slice(8 * k, 8 * k + 8)
        res = res_ref[rows, :]
        delta = res[None] - past_ref[:, rows, :]
        pieces.append(
            jnp.concatenate([delta.reshape(HIST * 8, LANES), res, fld_ref[rows, :]], axis=0)
        )
    wide = jnp.concatenate(pieces, axis=1)
    part = split_product(wide, wide, ((1,), (1,)))

    @pl.when(step == 0)
    def _():
        acc_ref[...] = part

    @pl.when(step > 0)
    def _():
        acc_ref[...] += part

    @pl.when(step == LINES // CHUNK - 1)
    def _():
        size = BANDS * 8
        same = (iota((size, size), 0) & 7) == (iota((size, size), 1) & 7)
        total = jnp.where(same, acc_ref[...], 0.0)
        columns = (iota((size, LANES), 0) >> 3 == iota((size, LANES), 1)).astype(F32)
        rows = (iota((24, size), 1) >> 3 == iota((24, size), 0)).astype(F32)
        folded = lax.dot(rows, lax.dot(total, columns, precision=EXACT), precision=EXACT)
        packed = (
            folded[0:8]
            + pltpu.roll(folded[8:16], 32, 1)
            + pltpu.roll(folded[16:24], 64, 1)
        )
        out_ref[...] = jnp.broadcast_to(packed[None], out_ref.shape)


def gram_partial(res, fld, past, copies):
    return pl.pallas_call(
        gram_kernel,
        grid=(LINES // CHUNK,),
        out_shape=jax.ShapeDtypeStruct((copies, 8, LANES), F32),
        in_specs=[
            pl.BlockSpec((CHUNK, LANES), lambda t: (t, 0)),
            pl.BlockSpec((CHUNK, LANES), lambda t: (t, 0)),
            pl.BlockSpec((HIST, CHUNK, LANES), lambda t: (0, t, 0)),
        ],
        out_specs=pl.BlockSpec((copies, 8, LANES), lambda t: (0, 0, 0)),
        scratch_shapes=[pltpu.VMEM((BANDS * 8, BANDS * 8), F32)],
        compiler_params=params(12),
        name="gram",
    )(res, fld, past)


def solve(packed):
    place = iota((24, LANES), 0)

    def column(i):
        parts = [
            jnp.broadcast_to(packed[:, 32 * b + i : 32 * b + i + 1], (8, LANES)) for b in range(3)
        ]
        return jnp.concatenate(parts, axis=0)

    rows = [column(i) for i in range(HIST)]
    right = column(HIST)
    trace = rows[0][0:1]
    for i in range(1, HIST):
        trace = trace + rows[i][i : i + 1]
    shift = (RIDGE / HIST) * trace + 1.0
    rows = [rows[i] + jnp.where(place == i, shift, 0.0) for i in range(HIST)]
    inverse = []
    for k in range(HIST):
        inv = 1.0 / rows[k][k : k + 1]
        inverse.append(inv)
        after = jnp.where(place > k, rows[k] * inv, 0.0)
        for i in range(k + 1, HIST):
            rows[i] = rows[i] - after * rows[i][k : k + 1]
        right = right - after * right[k : k + 1]
    coeffs = [None] * HIST
    for k in reversed(range(HIST)):
        coeffs[k] = right[k : k + 1] * inverse[k]
        right = right - jnp.where(place < k, rows[k] * coeffs[k], 0.0)
    remain = 1.0 - functools.reduce(jnp.add, coeffs)
    return remain, coeffs


def mix_kernel(sums_ref, res_ref, past_ref, mixed_ref, moment_ref, coeff_ref):
    packed = jnp.sum(sums_ref[...], axis=0)
    remain, coeffs = solve(packed)
    for i in range(HIST):
        coeff_ref[i : i + 1, :] = coeffs[i]
    coeff_ref[HIST : HIST + 1, :] = remain
    res_square = packed[4:5, 64 + HIST : 65 + HIST]
    fld_square = packed[5:6, 65 + HIST : 66 + HIST]
    coeff_ref[21:22, :] = jnp.broadcast_to(jnp.sqrt(res_square / (fld_square + 1.0)), (1, LANES))
    spread = [jnp.broadcast_to(c, (ROWS, LANES)) for c in coeffs]
    remain = jnp.broadcast_to(remain, (ROWS, LANES))
    rise = ramp((ROWS, LANES), 0, 1.0)
    fall = ramp((ROWS, LANES), 0, -1.0)
    for plane in range(2 * PLANES):
        rows = slice(ROWS * plane, ROWS * plane + ROWS)
        total = remain * res_ref[rows, :]
        for i in range(HIST):
            total = total + spread[i] * past_ref[i, rows, :]
        mixed_ref[rows, :] = total
        s, z = divmod(plane, PLANES)
        moment_ref[0, s, z : z + 1, :] = jnp.sum(rise * total, axis=0, keepdims=True)
        moment_ref[0, 2 + s, z : z + 1, :] = jnp.sum(fall * total, axis=0, keepdims=True)
    for k in range(1, moment_ref.shape[0]):
        moment_ref[k] = moment_ref[0]


def mix(sums, res, past, copies):
    return pl.pallas_call(
        mix_kernel,
        out_shape=(
            jax.ShapeDtypeStruct((LINES, LANES), F32),
            jax.ShapeDtypeStruct((copies, 4, PLANES, LANES), F32),
            jax.ShapeDtypeStruct((24, LANES), F32),
        ),
        in_specs=[VMEM] * 3,
        out_specs=(VMEM,) * 3,
        compiler_params=params(16),
        name="mix",
    )(sums, res, past)


def local_kernel(coeff_ref, fld_ref, past_ref, mixed_ref, base_ref, moment_ref, near_ref):
    wide = jnp.concatenate(
        [mixed_ref[ROWS * k : ROWS * k + ROWS, :] for k in range(2 * PLANES)], axis=1
    )
    near = split_product(near_matrix(ROWS), wide, ((1,), (0,)))
    for k in range(2 * PLANES):
        near_ref[ROWS * k : ROWS * k + ROWS, :] = near[:, LANES * k : LANES * k + LANES]
    coeffs = [jnp.broadcast_to(coeff_ref[i : i + 1, :], (ROWS, LANES)) for i in range(HIST + 1)]
    peak = jnp.zeros((ROWS, LANES), F32)
    for s in range(2):
        planes = [near_ref[ROWS * k : ROWS * k + ROWS, :] for k in range(PLANES * s, PLANES * s + PLANES)]
        rising = planes[0]
        falling = planes[0]
        for z in range(1, PLANES):
            rising = rising + math.exp(z / DECAY) * planes[z]
            falling = falling + math.exp(-z / DECAY) * planes[z]
        moment_ref[s] = rising
        moment_ref[2 + s] = falling
        for z in range(PLANES):
            rows = slice(ROWS * (PLANES * s + z), ROWS * (PLANES * s + z) + ROWS)
            own = mixed_ref[rows, :]
            peak = jnp.maximum(peak, jnp.abs(own))
            total = STEP_LOCAL * own + coeffs[HIST] * fld_ref[rows, :]
            for i in range(HIST):
                total = total + coeffs[i] * past_ref[i, rows, :]
            for z2 in range(PLANES):
                total = total + near_value(abs(z - z2)) * planes[z2]
            base_ref[rows, :] = total
    moment_ref[4] = peak


def local_part(coeffs, fld, past, mixed):
    return pl.pallas_call(
        local_kernel,
        out_shape=(
            jax.ShapeDtypeStruct((LINES, LANES), F32),
            jax.ShapeDtypeStruct((5, ROWS, LANES), F32),
        ),
        in_specs=[VMEM] * 4,
        out_specs=(VMEM,) * 2,
        scratch_shapes=[pltpu.VMEM((LINES, LANES), F32)],
        compiler_params=params(16),
        name="local_part",
    )(coeffs, fld, past, mixed)


def column_kernel(ends_ref, base_ref, moment_ref, full_ref, send_ref):
    here = lax.axis_index("gy")
    count = ends_ref.shape[0]
    shape = (count, LANES)
    other = iota(shape, 0)
    down = far_weight(jnp.full(shape, here, jnp.int32), other, ROWS)
    up = far_weight(other, jnp.full(shape, here, jnp.int32), ROWS)
    fields = []
    for kind, weight in ((0, down), (2, up)):
        for s in range(2):
            total = weight[0:1] * ends_ref[0, kind + s]
            for q in range(1, count):
                total = total + weight[q : q + 1] * ends_ref[q, kind + s]
            fields.append(total)
    wide = jnp.concatenate(fields, axis=1)
    row = iota((16, PLANES), 0)
    col = iota((16, PLANES), 1)
    lag = (0.5 * LENGTH - jnp.abs(row - col).astype(F32)) / DECAY
    near = (jnp.exp(lag) + jnp.exp(-lag)) * (0.5 / TOTAL)
    rise = jnp.exp(col.astype(F32) / DECAY)
    fall = jnp.exp(col.astype(F32) / -DECAY)
    mixer = jnp.where(row < 8, near, jnp.where(row == 8, rise, fall))
    smooth = lax.dot(mixer, wide, precision=EXACT)

    fall_y = ramp((ROWS, LANES), 0, -1.0)
    rise_y = ramp((ROWS, LANES), 0, 1.0)

    def spread(line, s):
        return (
            fall_y * smooth[line : line + 1, LANES * s : LANES * s + LANES]
            + rise_y * smooth[line : line + 1, LANES * (2 + s) : LANES * (2 + s) + LANES]
        )

    def put(k, value):
        send_ref[pl.ds(k, ROWS, stride=8), :] = value

    for s in range(2):
        put(s, moment_ref[s] + spread(8, s))
        put(2 + s, moment_ref[2 + s] + spread(9, s))
    first = jnp.zeros((ROWS, LANES), F32)
    second = jnp.zeros((ROWS, LANES), F32)
    energy = jnp.zeros((ROWS, LANES), F32)
    for z in range(PLANES):
        pair = []
        for s in range(2):
            rows = slice(ROWS * (PLANES * s + z), ROWS * (PLANES * s + z) + ROWS)
            value = base_ref[rows, :] + spread(z, s)
            full_ref[rows, :] = value
            pair.append(value)
        gap = pair[0] - pair[1]
        first = first + math.exp(-z / DECAY) * gap
        second = second + math.exp(z / DECAY) * gap
        energy = energy + (gap * gap * (1.0 / (4.0 * CHI_N)) - 0.5 * (pair[0] + pair[1]))
    put(4, first)
    put(5, second)
    put(6, energy)
    put(7, moment_ref[4])


def column_part(ends, base, moments, owners):
    return pl.pallas_call(
        column_kernel,
        out_shape=(
            jax.ShapeDtypeStruct((LINES, LANES), F32),
            jax.ShapeDtypeStruct((owners * 8, LANES), F32),
        ),
        in_specs=[VMEM] * 3,
        out_specs=(VMEM,) * 2,
        compiler_params=params(8),
        name="column_part",
    )(ends, base, moments)


def owner_kernel(got_ref, send_ref):
    count = got_ref.shape[0] // 8
    take = lambda k: got_ref[pl.ds(k, count, stride=8), :]
    row = iota((count, count), 0)
    col = iota((count, count), 1)
    rising = jnp.concatenate([take(0), take(1)], axis=1)
    falling = jnp.concatenate([take(2), take(3)], axis=1)
    down = split_product(far_weight(row, col, PLANES), rising, ((1,), (0,)))
    up = split_product(far_weight(col, row, PLANES), falling, ((1,), (0,)))
    down = (down[:, :LANES], down[:, LANES:])
    up = (up[:, :LANES], up[:, LANES:])
    fall_sum = sum(math.exp(-z / DECAY) for z in range(PLANES))
    rise_sum = sum(math.exp(z / DECAY) for z in range(PLANES))
    fall_square = sum(math.exp(-2.0 * z / DECAY) for z in range(PLANES))
    rise_square = sum(math.exp(2.0 * z / DECAY) for z in range(PLANES))
    a = down[0] - down[1]
    b = up[0] - up[1]
    square = (
        a * (2.0 * take(4) + fall_square * a + (2.0 * PLANES) * b)
        + b * (2.0 * take(5) + rise_square * b)
    )
    energy = (
        take(6)
        + square * (1.0 / (4.0 * CHI_N))
        - 0.5 * (fall_sum * (down[0] + down[1]) + rise_sum * (up[0] + up[1]))
    )
    energy = jnp.sum(energy, axis=0, keepdims=True)
    peak = jnp.max(take(7), axis=0, keepdims=True)
    values = (*down, *up, energy, peak, peak, peak)
    for k, value in enumerate(values):
        send_ref[pl.ds(k, count, stride=8), :] = jnp.broadcast_to(value, (count, LANES))


def owner_part(got):
    return pl.pallas_call(
        owner_kernel,
        out_shape=jax.ShapeDtypeStruct(got.shape, F32),
        in_specs=[VMEM],
        out_specs=VMEM,
        compiler_params=params(8),
        name="owner_part",
    )(got)


def tally_kernel(got_ref, out_ref):
    energy = jnp.sum(got_ref[pl.ds(4, ROWS, stride=8), :], axis=0, keepdims=True)
    peak = jnp.max(got_ref[pl.ds(5, ROWS, stride=8), :], axis=0, keepdims=True)
    value = jnp.where(iota((8, LANES), 0) == 0, energy, peak)
    out_ref[...] = jnp.broadcast_to(value[None], out_ref.shape)


def tally(got, copies):
    return pl.pallas_call(
        tally_kernel,
        out_shape=jax.ShapeDtypeStruct((copies, 8, LANES), F32),
        in_specs=[VMEM],
        out_specs=VMEM,
        compiler_params=params(8),
        name="tally",
    )(got)


def finish_kernel(got_ref, full_ref, out_ref):
    down = [got_ref[pl.ds(s, ROWS, stride=8), :] for s in range(2)]
    up = [got_ref[pl.ds(2 + s, ROWS, stride=8), :] for s in range(2)]
    for s in range(2):
        for z in range(PLANES):
            rows = slice(ROWS * (PLANES * s + z), ROWS * (PLANES * s + z) + ROWS)
            out_ref[rows, :] = (
                full_ref[rows, :]
                + math.exp(-z / DECAY) * down[s]
                + math.exp(z / DECAY) * up[s]
            )


def finish(got, full):
    return pl.pallas_call(
        finish_kernel,
        out_shape=jax.ShapeDtypeStruct((LINES, LANES), F32),
        in_specs=[VMEM] * 2,
        out_specs=VMEM,
        compiler_params=params(8),
        name="finish",
    )(got, full)


def summary_kernel(got_ref, coeff_ref, out_ref):
    energy = jnp.sum(got_ref[:, 0, :]) * (1.0 / CELLS)
    out_ref[0] = energy
    out_ref[1] = jnp.max(coeff_ref[21:22, :])
    out_ref[2] = jnp.max(got_ref[:, 1, :])


def summarize(got, coeffs):
    return pl.pallas_call(
        summary_kernel,
        out_shape=jax.ShapeDtypeStruct((3,), F32),
        in_specs=[VMEM] * 2,
        out_specs=pl.BlockSpec(memory_space=pltpu.SMEM),
        compiler_params=params(8),
        name="summary",
    )(got, coeffs)


def swap(x, axis):
    return lax.all_to_all(x, axis, 0, 0, tiled=True)


def shards(fields, residual, past_fields, past_residuals):
    slabs = lax.axis_size("gz")
    pencils = lax.axis_size("gy")
    res = residual.reshape(LINES, LANES)
    fld = fields.reshape(LINES, LANES)
    past_res = past_residuals.reshape(HIST, LINES, LANES)
    past_fld = past_fields.reshape(HIST, LINES, LANES)
    sums = jnp.sum(swap(gram_partial(res, fld, past_res, slabs), "gz"), axis=0)
    sums = swap(jnp.broadcast_to(sums[None], (pencils, 8, LANES)), "gy")
    mixed, ends, coeffs = mix(sums, res, past_res, pencils)
    ends = swap(ends, "gy")
    base, moments = local_part(coeffs, fld, past_fld, mixed)
    full, send = column_part(ends, base, moments, slabs)
    got = swap(send.reshape(slabs, 8, LANES), "gz")
    send = owner_part(got.reshape(slabs * 8, LANES))
    got = swap(send.reshape(slabs, 8, LANES), "gz").reshape(slabs * 8, LANES)
    last = swap(tally(got, pencils), "gy")
    new_fields = finish(got, full)
    return new_fields.reshape(fields.shape), summarize(last, coeffs)


def solution(mesh):
    placed = (
        P(None, "gz", "gy", None),
        P(None, "gz", "gy", None),
        P(None, None, "gz", "gy", None),
        P(None, None, "gz", "gy", None),
    )
    return jax.shard_map(
        shards, mesh=mesh, in_specs=placed, out_specs=(P(None, "gz", "gy", None), P()), check_vma=False
    )
```

time: 210 us -> 94.2 us (0.45)
  blocking collectives: 111 us -> 57 us
  matrix products: 38.7 us -> 0 us
  other arithmetic: 16.1 us -> 0.04 us
  Pallas kernels: 0 us -> 10.1 us
  starting transfers between devices: 17.7 us -> 10.8 us
  between operations: 6.67 us -> 0.68 us
  waiting for transfers between devices: 10.3 us -> 5.7 us
    psum x4 -> x0, blocking collectives: 71.4 us -> none  [by_axis(): return functools.reduce(lax.psum, axes, shard)]
    all_to_all x0 -> x4, blocking collectives: none -> 57 us  [swap(): return lax.all_to_all(x, axis, 0, 0, tiled=True)]
    unnamed x4 -> x0, blocking collectives: 39.2 us -> none
    dot_general x8 -> x0, matrix products: 37.8 us -> none  [the longest x1 9.13 us: shards(): jnp.dot(coeffs, past_rows, precision=EXACT, preferred_element_type=jnp.fl...]
    pallas_call x0 -> x8, Pallas kernels: none -> 10.1 us  [the longest x1 5 us: gram_partial(): pl.pallas_call(gram_kernel, grid=(LINES // CHUNK,), out_shape=jax.ShapeDt...]
    all_to_all x3 -> x2, starting transfers between devices: 17.7 us -> 10.8 us  [swap(): return lax.all_to_all(x, axis, 0, 0, tiled=True)]
    another operation x6 -> x0, other arithmetic: 5.26 us -> none  [the longest x3 2.49 us: shards(): factor = jnp.linalg.cholesky(system)]
    unnamed x6 -> x0, other arithmetic: 4.87 us -> none
  transfers between devices with their start and end apart: 3 -> 2, of which waited for: 3 -> 2; matrix products, arithmetic and copies ran while one was open for 7% -> 0% of each run, Pallas kernels for 0% -> 2%
where the time goes in v1:
time: 94.2 us; the launch traced here: 93.7 us
  blocking collectives  57 us (61%)
  starting transfers between devices  10.8 us (11%)
  Pallas kernels  10.1 us (11%)
  local copies, waits for them, and re-layouts  9.37 us (10%)
  waiting for transfers between devices  5.7 us (6%)
    all_to_all x4, blocking collectives, swap(): return lax.all_to_all(x, axis, 0, 0, tiled=True)  57 us
    all_to_all x2, starting transfers between devices, swap(): return lax.all_to_all(x, axis, 0, 0, tiled=True)  10.8 us
    unnamed x14, local copies, waits for them, and re-layouts  9.36 us
    all_to_all x2, waiting for transfers between devices, swap(): return lax.all_to_all(x, axis, 0, 0, tiled=True)  5.7 us
    pallas_call x1, Pallas kernels, gram_partial(): pl.pallas_call(gram_kernel, grid=(LINES // CHUNK,), out_shape=jax.ShapeDt...  5 us
  transfers between devices with their start and end apart: 2, of which 2 were waited for; matrix products, arithmetic and copies ran while one was open for 0% of the time, Pallas kernels for 2%

profile of v1, /device:TPU:1, one launch (start us, length us, event | category | flops | bytes accessed | tf_op | source)
XLA Modules:
  0.0 93.7 jit_solution(1165665813970964969)
XLA Ops:
  0.6 0.0 copy-start
  0.6 2.5 %copy-done = f32[20,2,8,32,128]{4,3,2,1,0:T(8,128)S(1)} copy-done((f32[20,2,8,32,128]{4,3,2,1,0:T(8,128)S(1)}, f32[20,2,8,32,128]{4,3,2,1,0:T(8,128)}, u32[]{:S(2)}) %copy-start) | copy-done | bytes 5242904
  3.1 0.9 %copy-done.3 = f32[2,8,32,128]{3,2,1,0:T(8,128)S(1)} copy-done((f32[2,8,32,128]{3,2,1,0:T(8,128)S(1)}, f32[2,8,32,128]{3,2,1,0:T(8,128)}, u32[]{:S(2)}) %copy-start.3) | copy-done | bytes 262168
  4.1 0.9 %copy-done.5 = f32[2,8,32,128]{3,2,1,0:T(8,128)S(1)} copy-done((f32[2,8,32,128]{3,2,1,0:T(8,128)S(1)}, f32[2,8,32,128]{3,2,1,0:T(8,128)}, u32[]{:S(2)}) %copy-start.5) | copy-done | bytes 262168
  5.0 5.0 %gram.1 = f32[32,8,128]{2,1,0:T(8,128)S(1)} custom-call(f32[512,128]{1,0:T(8,128)S(1)} %bitcast.16, f32[512,128]{1,0:T(8,128)S(1)} %bitcast.14, f32[20,512,128]{2,1,0:T(8,128)S(1)} %bitcast.9), custom_call_target="tpu_custom_call" | custom-call | tf_op jit(solution)/shard_map/gram/pallas_call | solution.py:119
  10.0 20.8 %all_to_all.30 = f32[32,8,128]{2,1,0:T(8,128)S(1)} all-to-all(f32[32,8,128]{2,1,0:T(8,128)S(1)} %gram.1), channel_id=1, replica_groups=mesh['gz'=32,'gy'=8] {'gz'}, dimensions={0} | all-to-all | bytes 262144 | tf_op jit(solution)/shard_map/all_to_all | solution.py:432
  30.9 11.1 %all_to_all.31.sums_ref = f32[8,8,128]{2,1,0:T(8,128)S(1)} all-to-all(f32[8,8,128]{2,1,0:T(8,128)S(1)} %broadcast_in_dim.2), channel_id=1, replica_groups=mesh['gz'=32,'gy'=8] {'gy'}, dimensions={0} | all-to-all | bytes 65536 | tf_op jit(solution)/shard_map/all_to_all | solution.py:432
  41.9 0.0 copy-done.6
  41.9 2.5 %copy-done.1 = f32[20,2,8,32,128]{4,3,2,1,0:T(8,128)S(1)} copy-done((f32[20,2,8,32,128]{4,3,2,1,0:T(8,128)S(1)}, f32[20,2,8,32,128]{4,3,2,1,0:T(8,128)}, u32[]{:S(2)}) %copy-start.1) | copy-done | bytes 5242904
  44.4 1.5 %mix.1 = (f32[512,128]{1,0:T(8,128)S(1)}, f32[8,4,8,128]{3,2,1,0:T(8,128)}, f32[24,128]{1,0:T(8,128)S(1)}) custom-call(f32[8,8,128]{2,1,0:T(8,128)S(1)} %all_to_all.31.sums_ref, f32[512,128]{1,0:T(8,128)S(1)} %bitcast.17, f32[20,512,128]{2,1,0:T(8,128)S(1)} %bitcast.10), custom_call_target="tpu_custom_call" | custom-call | tf_op jit(solution)/shard_map/mix/pallas_call | solution.py:194
  46.0 4.0 %all-to-all-start.2 = ((f32[8,4,8,128]{3,2,1,0:T(8,128)}), f32[8,4,8,128]{3,2,1,0:T(8,128)S(1)}, u32[]{:S(2)}, u32[]{:S(2)}) async-start(f32[8,4,8,128]{3,2,1,0:T(8,128)} %get-tuple-element.9), calls=%async_computation.2 | async-start | bytes 262144 | tf_op jit(solution)/shard_map/all_to_all | solution.py:432
  50.0 0.0 copy-done.4
  50.0 2.5 %copy-done.2 = f32[20,2,8,32,128]{4,3,2,1,0:T(8,128)S(1)} copy-done((f32[20,2,8,32,128]{4,3,2,1,0:T(8,128)S(1)}, f32[20,2,8,32,128]{4,3,2,1,0:T(8,128)}, u32[]{:S(2)}) %copy-start.2) | copy-done | bytes 5242904
  52.5 1.1 %local_part.1 = (f32[512,128]{1,0:T(8,128)S(1)}, f32[5,32,128]{2,1,0:T(8,128)S(1)}) custom-call(f32[24,128]{1,0:T(8,128)S(1)} %get-tuple-element.10.coeff_ref, f32[512,128]{1,0:T(8,128)S(1)} %bitcast.15, f32[20,512,128]{2,1,0:T(8,128)S(1)} %bitcast.11, f32[512,128]{1,0:T(8,128)S(1)} %get-tuple-element.11.mixed_ref), custom_call_target="tpu_custom_call" | custom-call | tf_op jit(solution)/shard_map/local_part/pallas_call | solution.py:240
  53.5 1.7 %all-to-all-done.2.ends_ref = f32[8,4,8,128]{3,2,1,0:T(8,128)S(1)} async-done(((f32[8,4,8,128]{3,2,1,0:T(8,128)}), f32[8,4,8,128]{3,2,1,0:T(8,128)S(1)}, u32[]{:S(2)}, u32[]{:S(2)}) %all-to-all-start.2) | async-done | bytes 131104 | tf_op jit(solution)/shard_map/all_to_all | solution.py:432
  55.2 0.3 column_part.1
  55.5 12.5 %all_to_all.32 = f32[32,8,128]{2,1,0:T(8,128)S(1)} all-to-all(f32[32,8,128]{2,1,0:T(8,128)S(1)} %bitcast.20), channel_id=1, replica_groups=mesh['gz'=32,'gy'=8] {'gz'}, dimensions={0} | all-to-all | bytes 262144 | tf_op jit(solution)/shard_map/all_to_all | solution.py:432
  68.0 0.2 owner_part.1
  68.2 12.7 %all_to_all.33 = f32[32,8,128]{2,1,0:T(8,128)S(1)} all-to-all(f32[32,8,128]{2,1,0:T(8,128)S(1)} %bitcast.19), channel_id=1, replica_groups=mesh['gz'=32,'gy'=8] {'gz'}, dimensions={0} | all-to-all | bytes 262144 | tf_op jit(solution)/shard_map/all_to_all | solution.py:432
  80.9 0.6 tally.1
  81.5 6.8 %all-to-all-start.5 = ((f32[8,8,128]{2,1,0:T(8,128)}), f32[8,8,128]{2,1,0:T(8,128)S(1)}, u32[]{:S(2)}, u32[]{:S(2)}) async-start(f32[8,8,128]{2,1,0:T(8,128)} %tally.1), calls=%async_computation.5 | async-start | bytes 65536 | tf_op jit(solution)/shard_map/all_to_all | solution.py:432
  88.3 0.7 finish.1
  89.0 4.0 %all-to-all-done.5.got_ref = f32[8,8,128]{2,1,0:T(8,128)S(1)} async-done(((f32[8,8,128]{2,1,0:T(8,128)}), f32[8,8,128]{2,1,0:T(8,128)S(1)}, u32[]{:S(2)}, u32[]{:S(2)}) %all-to-all-start.5) | async-done | bytes 32800 | tf_op jit(solution)/shard_map/all_to_all | solution.py:432
  93.0 0.6 summary.1
  (8 shorter events, 0.1 us)
Async XLA Ops:
  0.6 2.5 %copy-start = (f32[20,2,8,32,128]{4,3,2,1,0:T(8,128)S(1)}, f32[20,2,8,32,128]{4,3,2,1,0:T(8,128)}, u32[]{:S(2)}) copy-start(f32[20,2,8,32,128]{4,3,2,1,0:T(8,128)} %param.7) | copy-start | bytes 15728644
  3.1 0.9 %copy-start.3 = (f32[2,8,32,128]{3,2,1,0:T(8,128)S(1)}, f32[2,8,32,128]{3,2,1,0:T(8,128)}, u32[]{:S(2)}) copy-start(f32[2,8,32,128]{3,2,1,0:T(8,128)} %param.4) | copy-start | bytes 786436
  4.1 0.9 %copy-start.5 = (f32[2,8,32,128]{3,2,1,0:T(8,128)S(1)}, f32[2,8,32,128]{3,2,1,0:T(8,128)}, u32[]{:S(2)}) copy-start(f32[2,8,32,128]{3,2,1,0:T(8,128)} %param.5) | copy-start | bytes 786436
  5.0 36.9 %copy-start.6 = (f32[2,8,32,128]{3,2,1,0:T(8,128)S(1)}, f32[2,8,32,128]{3,2,1,0:T(8,128)}, u32[]{:S(2)}) copy-start(f32[2,8,32,128]{3,2,1,0:T(8,128)} %param.5) | copy-start | bytes 786436
  5.0 45.0 %copy-start.4 = (f32[2,8,32,128]{3,2,1,0:T(8,128)S(1)}, f32[2,8,32,128]{3,2,1,0:T(8,128)}, u32[]{:S(2)}) copy-start(f32[2,8,32,128]{3,2,1,0:T(8,128)} %param.4) | copy-start | bytes 786436
  41.9 2.5 %copy-start.1 = (f32[20,2,8,32,128]{4,3,2,1,0:T(8,128)S(1)}, f32[20,2,8,32,128]{4,3,2,1,0:T(8,128)}, u32[]{:S(2)}) copy-start(f32[20,2,8,32,128]{4,3,2,1,0:T(8,128)} %param.7) | copy-start | bytes 15728644
  46.0 9.3 %all-to-all-start.2 = ((f32[8,4,8,128]{3,2,1,0:T(8,128)}), f32[8,4,8,128]{3,2,1,0:T(8,128)S(1)}, u32[]{:S(2)}, u32[]{:S(2)}) async-start(f32[8,4,8,128]{3,2,1,0:T(8,128)} %get-tuple-element.9), calls=%async_computation.2 | async-start | bytes 262144 | tf_op jit(solution)/shard_map/all_to_all | solution.py:432
  50.0 2.5 %copy-start.2 = (f32[20,2,8,32,128]{4,3,2,1,0:T(8,128)S(1)}, f32[20,2,8,32,128]{4,3,2,1,0:T(8,128)}, u32[]{:S(2)}) copy-start(f32[20,2,8,32,128]{4,3,2,1,0:T(8,128)} %param.6) | copy-start | bytes 15728644
  81.5 11.5 %all-to-all-start.5 = ((f32[8,8,128]{2,1,0:T(8,128)}), f32[8,8,128]{2,1,0:T(8,128)S(1)}, u32[]{:S(2)}, u32[]{:S(2)}) async-start(f32[8,8,128]{2,1,0:T(8,128)} %tally.1), calls=%async_computation.5 | async-start | bytes 65536 | tf_op jit(solution)/shard_map/all_to_all | solution.py:432

commit v2 on v1

--- a/solution.py
+++ b/solution.py
@@ -28,6 +28,7 @@
 CELLS = 256 * 256 * 128
 
 VMEM = pl.BlockSpec(memory_space=pltpu.VMEM)
+HBM = pl.BlockSpec(memory_space=pltpu.HBM)
 
 
 def params(mib, **more):
@@ -78,58 +79,103 @@
     return jnp.where(col < row, below, jnp.where(col > row, above, 0.0))
 
 
-def gram_kernel(res_ref, fld_ref, past_ref, out_ref, acc_ref):
-    step = pl.program_id(0)
-    pieces = []
-    for k in range(CHUNK // 8):
-        rows = slice(8 * k, 8 * k + 8)
-        res = res_ref[rows, :]
-        delta = res[None] - past_ref[:, rows, :]
-        pieces.append(
-            jnp.concatenate([delta.reshape(HIST * 8, LANES), res, fld_ref[rows, :]], axis=0)
-        )
-    wide = jnp.concatenate(pieces, axis=1)
-    part = split_product(wide, wide, ((1,), (1,)))
-
-    @pl.when(step == 0)
-    def _():
-        acc_ref[...] = part
-
-    @pl.when(step > 0)
-    def _():
-        acc_ref[...] += part
-
-    @pl.when(step == LINES // CHUNK - 1)
-    def _():
-        size = BANDS * 8
-        same = (iota((size, size), 0) & 7) == (iota((size, size), 1) & 7)
-        total = jnp.where(same, acc_ref[...], 0.0)
-        columns = (iota((size, LANES), 0) >> 3 == iota((size, LANES), 1)).astype(F32)
-        rows = (iota((24, size), 1) >> 3 == iota((24, size), 0)).astype(F32)
-        folded = lax.dot(rows, lax.dot(total, columns, precision=EXACT), precision=EXACT)
-        packed = (
-            folded[0:8]
-            + pltpu.roll(folded[8:16], 32, 1)
-            + pltpu.roll(folded[16:24], 64, 1)
-        )
-        out_ref[...] = jnp.broadcast_to(packed[None], out_ref.shape)
+def gram_kernel(res_any, fld_any, past_any, out_ref, res_ref, past_ref, fld_ref, high_ref, low_ref, acc_ref, sems):
+    steps = LINES // CHUNK
+    copies = [
+        pltpu.make_async_copy(res_any, res_ref, sems.at[steps]),
+        pltpu.make_async_copy(fld_any, fld_ref, sems.at[steps + 1]),
+    ]
+    chunks = []
+    for t in range(steps):
+        rows = pl.ds(CHUNK * t, CHUNK)
+        chunks.append(pltpu.make_async_copy(past_any.at[:, rows], past_ref.at[:, rows], sems.at[t]))
+    for copy in copies + chunks:
+        copy.start()
+    for copy in copies:
+        copy.wait()
+
+    def split(t):
+        for k in range(CHUNK // 8):
+            rows = slice(CHUNK * t + 8 * k, CHUNK * t + 8 * k + 8)
+            res = res_ref[rows, :]
+            delta = res[None] - past_ref[:, rows, :]
+            band = jnp.concatenate(
+                [delta.reshape(HIST * 8, LANES), res, fld_ref[rows, :]], axis=0
+            )
+            columns = slice(LANES * k, LANES * k + LANES)
+            high_ref[t % 2, :, columns], low_ref[t % 2, :, columns] = halves(band)
+
+    def multiply(t):
+        high = high_ref[t % 2]
+        low = low_ref[t % 2]
+        for k, part in enumerate((high, low)):
+            value = product(high, part, ((1,), (1,)))
+            if t == 0:
+                acc_ref[k] = value
+            else:
+                acc_ref[k] += value
+
+    chunks[0].wait()
+    split(0)
+    for t in range(steps):
+        if t + 1 < steps:
+            chunks[t + 1].wait()
+            split(t + 1)
+        multiply(t)
+
+    size = BANDS * 8
+    same = (iota((size, size), 0) & 7) == (iota((size, size), 1) & 7)
+    major = jnp.where(same, acc_ref[0] + acc_ref[1], 0.0)
+    minor = jnp.where(same, acc_ref[1], 0.0)
+    columns = (iota((size, LANES), 0) >> 3 == iota((size, LANES), 1)).astype(F32)
+    rows = (iota((24, size), 1) >> 3 == iota((24, size), 0)).astype(F32)
+    half = lax.dot(rows, major, precision=EXACT) + lax.dot_general(
+        rows, minor, (((1,), (1,)), ((), ())), precision=EXACT
+    )
+    folded = lax.dot(half, columns, precision=EXACT)
+    packed = (
+        folded[0:8] + pltpu.roll(folded[8:16], 32, 1) + pltpu.roll(folded[16:24], 64, 1)
+    )
+    out_ref[...] = jnp.broadcast_to(packed[None], out_ref.shape)
 
 
 def gram_partial(res, fld, past, copies):
+    wide = (CHUNK // 8) * LANES
     return pl.pallas_call(
         gram_kernel,
-        grid=(LINES // CHUNK,),
+        out_shape=(
+            jax.ShapeDtypeStruct((copies, 8, LANES), F32),
+            pltpu.VMEM((LINES, LANES), F32),
+            pltpu.VMEM((HIST, LINES, LANES), F32),
+        ),
+        in_specs=[HBM] * 3,
+        out_specs=(VMEM,) * 3,
+        scratch_shapes=[
+            pltpu.VMEM((LINES, LANES), F32),
+            pltpu.VMEM((2, BANDS * 8, wide), BF16),
+            pltpu.VMEM((2, BANDS * 8, wide), BF16),
+            pltpu.VMEM((2, BANDS * 8, BANDS * 8), F32),
+            pltpu.SemaphoreType.DMA((LINES // CHUNK + 2,)),
+        ],
+        compiler_params=params(54),
+        name="gram",
+    )(*(pltpu.with_memory_space_constraint(x, pltpu.HBM) for x in (res, fld, past)))
+
+
+def relay_kernel(got_ref, out_ref):
+    total = jnp.sum(got_ref[...], axis=0)
+    out_ref[...] = jnp.broadcast_to(total[None], out_ref.shape)
+
+
+def relay(got, copies):
+    return pl.pallas_call(
+        relay_kernel,
         out_shape=jax.ShapeDtypeStruct((copies, 8, LANES), F32),
-        in_specs=[
-            pl.BlockSpec((CHUNK, LANES), lambda t: (t, 0)),
-            pl.BlockSpec((CHUNK, LANES), lambda t: (t, 0)),
-            pl.BlockSpec((HIST, CHUNK, LANES), lambda t: (0, t, 0)),
-        ],
-        out_specs=pl.BlockSpec((copies, 8, LANES), lambda t: (0, 0, 0)),
-        scratch_shapes=[pltpu.VMEM((BANDS * 8, BANDS * 8), F32)],
-        compiler_params=params(12),
-        name="gram",
-    )(res, fld, past)
+        in_specs=[VMEM],
+        out_specs=VMEM,
+        compiler_params=params(4),
+        name="relay",
+    )(got)
 
 
 def solve(packed):
@@ -164,58 +210,39 @@
     return remain, coeffs
 
 
-def mix_kernel(sums_ref, res_ref, past_ref, mixed_ref, moment_ref, coeff_ref):
+def mix_kernel(
+    sums_ref, res_ref, past_ref, fld_ref, past_fld_ref,
+    end_ref, ratio_ref, base_ref, moment_ref, mixed_ref, near_ref,
+):
     packed = jnp.sum(sums_ref[...], axis=0)
     remain, coeffs = solve(packed)
-    for i in range(HIST):
-        coeff_ref[i : i + 1, :] = coeffs[i]
-    coeff_ref[HIST : HIST + 1, :] = remain
     res_square = packed[4:5, 64 + HIST : 65 + HIST]
     fld_square = packed[5:6, 65 + HIST : 66 + HIST]
-    coeff_ref[21:22, :] = jnp.broadcast_to(jnp.sqrt(res_square / (fld_square + 1.0)), (1, LANES))
-    spread = [jnp.broadcast_to(c, (ROWS, LANES)) for c in coeffs]
+    ratio = jnp.sqrt(res_square / (fld_square + 1.0))
+    ratio_ref[...] = jnp.broadcast_to(ratio, ratio_ref.shape)
+    coeffs = [jnp.broadcast_to(c, (ROWS, LANES)) for c in coeffs]
     remain = jnp.broadcast_to(remain, (ROWS, LANES))
     rise = ramp((ROWS, LANES), 0, 1.0)
     fall = ramp((ROWS, LANES), 0, -1.0)
+    peak = jnp.zeros((ROWS, LANES), F32)
     for plane in range(2 * PLANES):
         rows = slice(ROWS * plane, ROWS * plane + ROWS)
         total = remain * res_ref[rows, :]
         for i in range(HIST):
-            total = total + spread[i] * past_ref[i, rows, :]
-        mixed_ref[rows, :] = total
+            total = total + coeffs[i] * past_ref[i, rows, :]
+        mixed_ref[:, LANES * plane : LANES * plane + LANES] = total
+        peak = jnp.maximum(peak, jnp.abs(total))
         s, z = divmod(plane, PLANES)
-        moment_ref[0, s, z : z + 1, :] = jnp.sum(rise * total, axis=0, keepdims=True)
-        moment_ref[0, 2 + s, z : z + 1, :] = jnp.sum(fall * total, axis=0, keepdims=True)
-    for k in range(1, moment_ref.shape[0]):
-        moment_ref[k] = moment_ref[0]
-
-
-def mix(sums, res, past, copies):
-    return pl.pallas_call(
-        mix_kernel,
-        out_shape=(
-            jax.ShapeDtypeStruct((LINES, LANES), F32),
-            jax.ShapeDtypeStruct((copies, 4, PLANES, LANES), F32),
-            jax.ShapeDtypeStruct((24, LANES), F32),
-        ),
-        in_specs=[VMEM] * 3,
-        out_specs=(VMEM,) * 3,
-        compiler_params=params(16),
-        name="mix",
-    )(sums, res, past)
-
-
-def local_kernel(coeff_ref, fld_ref, past_ref, mixed_ref, base_ref, moment_ref, near_ref):
-    wide = jnp.concatenate(
-        [mixed_ref[ROWS * k : ROWS * k + ROWS, :] for k in range(2 * PLANES)], axis=1
-    )
-    near = split_product(near_matrix(ROWS), wide, ((1,), (0,)))
-    for k in range(2 * PLANES):
-        near_ref[ROWS * k : ROWS * k + ROWS, :] = near[:, LANES * k : LANES * k + LANES]
-    coeffs = [jnp.broadcast_to(coeff_ref[i : i + 1, :], (ROWS, LANES)) for i in range(HIST + 1)]
-    peak = jnp.zeros((ROWS, LANES), F32)
+        end_ref[0, s, z : z + 1, :] = jnp.sum(rise * total, axis=0, keepdims=True)
+        end_ref[0, 2 + s, z : z + 1, :] = jnp.sum(fall * total, axis=0, keepdims=True)
+    for k in range(1, end_ref.shape[0]):
+        end_ref[k] = end_ref[0]
+    moment_ref[4] = peak
+
+    near_ref[...] = split_product(near_matrix(ROWS), mixed_ref[...], ((1,), (0,)))
     for s in range(2):
-        planes = [near_ref[ROWS * k : ROWS * k + ROWS, :] for k in range(PLANES * s, PLANES * s + PLANES)]
+        near = lambda z: near_ref[:, LANES * (PLANES * s + z) : LANES * (PLANES * s + z + 1)]
+        planes = [near(z) for z in range(PLANES)]
         rising = planes[0]
         falling = planes[0]
         for z in range(1, PLANES):
@@ -224,31 +251,35 @@
         moment_ref[s] = rising
         moment_ref[2 + s] = falling
         for z in range(PLANES):
-            rows = slice(ROWS * (PLANES * s + z), ROWS * (PLANES * s + z) + ROWS)
-            own = mixed_ref[rows, :]
-            peak = jnp.maximum(peak, jnp.abs(own))
-            total = STEP_LOCAL * own + coeffs[HIST] * fld_ref[rows, :]
+            plane = PLANES * s + z
+            rows = slice(ROWS * plane, ROWS * plane + ROWS)
+            total = STEP_LOCAL * mixed_ref[:, LANES * plane : LANES * plane + LANES]
+            total = total + remain * fld_ref[rows, :]
             for i in range(HIST):
-                total = total + coeffs[i] * past_ref[i, rows, :]
+                total = total + coeffs[i] * past_fld_ref[i, rows, :]
             for z2 in range(PLANES):
                 total = total + near_value(abs(z - z2)) * planes[z2]
             base_ref[rows, :] = total
-    moment_ref[4] = peak
-
-
-def local_part(coeffs, fld, past, mixed):
-    return pl.pallas_call(
-        local_kernel,
+
+
+def mix(sums, res, past, fld, past_fld, copies):
+    return pl.pallas_call(
+        mix_kernel,
         out_shape=(
+            jax.ShapeDtypeStruct((copies, 4, PLANES, LANES), F32),
+            jax.ShapeDtypeStruct((8, LANES), F32),
             jax.ShapeDtypeStruct((LINES, LANES), F32),
             jax.ShapeDtypeStruct((5, ROWS, LANES), F32),
         ),
-        in_specs=[VMEM] * 4,
-        out_specs=(VMEM,) * 2,
-        scratch_shapes=[pltpu.VMEM((LINES, LANES), F32)],
-        compiler_params=params(16),
-        name="local_part",
-    )(coeffs, fld, past, mixed)
+        in_specs=[VMEM] * 5,
+        out_specs=(VMEM,) * 4,
+        scratch_shapes=[
+            pltpu.VMEM((ROWS, 2 * PLANES * LANES), F32),
+            pltpu.VMEM((ROWS, 2 * PLANES * LANES), F32),
+        ],
+        compiler_params=params(14),
+        name="mix",
+    )(sums, res, past, fld, past_fld)
 
 
 def column_kernel(ends_ref, base_ref, moment_ref, full_ref, send_ref):
@@ -386,7 +417,7 @@
     )(got)
 
 
-def finish_kernel(got_ref, full_ref, out_ref):
+def finish_kernel(last_ref, got_ref, full_ref, ratio_ref, out_ref, summary_ref):
     down = [got_ref[pl.ds(s, ROWS, stride=8), :] for s in range(2)]
     up = [got_ref[pl.ds(2 + s, ROWS, stride=8), :] for s in range(2)]
     for s in range(2):
@@ -397,35 +428,23 @@
                 + math.exp(-z / DECAY) * down[s]
                 + math.exp(z / DECAY) * up[s]
             )
-
-
-def finish(got, full):
+    summary_ref[0] = jnp.sum(last_ref[:, 0, :]) * (1.0 / CELLS)
+    summary_ref[1] = jnp.max(ratio_ref[...])
+    summary_ref[2] = jnp.max(last_ref[:, 1, :])
+
+
+def finish(last, got, full, ratio):
     return pl.pallas_call(
         finish_kernel,
-        out_shape=jax.ShapeDtypeStruct((LINES, LANES), F32),
-        in_specs=[VMEM] * 2,
-        out_specs=VMEM,
+        out_shape=(
+            jax.ShapeDtypeStruct((LINES, LANES), F32),
+            jax.ShapeDtypeStruct((3,), F32),
+        ),
+        in_specs=[VMEM] * 4,
+        out_specs=(VMEM, pl.BlockSpec(memory_space=pltpu.SMEM)),
         compiler_params=params(8),
         name="finish",
-    )(got, full)
-
-
-def summary_kernel(got_ref, coeff_ref, out_ref):
-    energy = jnp.sum(got_ref[:, 0, :]) * (1.0 / CELLS)
-    out_ref[0] = energy
-    out_ref[1] = jnp.max(coeff_ref[21:22, :])
-    out_ref[2] = jnp.max(got_ref[:, 1, :])
-
-
-def summarize(got, coeffs):
-    return pl.pallas_call(
-        summary_kernel,
-        out_shape=jax.ShapeDtypeStruct((3,), F32),
-        in_specs=[VMEM] * 2,
-        out_specs=pl.BlockSpec(memory_space=pltpu.SMEM),
-        compiler_params=params(8),
-        name="summary",
-    )(got, coeffs)
+    )(last, got, full, ratio)
 
 
 def swap(x, axis):
@@ -439,18 +458,17 @@
     fld = fields.reshape(LINES, LANES)
     past_res = past_residuals.reshape(HIST, LINES, LANES)
     past_fld = past_fields.reshape(HIST, LINES, LANES)
-    sums = jnp.sum(swap(gram_partial(res, fld, past_res, slabs), "gz"), axis=0)
-    sums = swap(jnp.broadcast_to(sums[None], (pencils, 8, LANES)), "gy")
-    mixed, ends, coeffs = mix(sums, res, past_res, pencils)
+    sums, res, past_res = gram_partial(res, fld, past_res, slabs)
+    sums = swap(relay(swap(sums, "gz"), pencils), "gy")
+    ends, ratio, base, moments = mix(sums, res, past_res, fld, past_fld, pencils)
     ends = swap(ends, "gy")
-    base, moments = local_part(coeffs, fld, past_fld, mixed)
     full, send = column_part(ends, base, moments, slabs)
     got = swap(send.reshape(slabs, 8, LANES), "gz")
     send = owner_part(got.reshape(slabs * 8, LANES))
     got = swap(send.reshape(slabs, 8, LANES), "gz").reshape(slabs * 8, LANES)
     last = swap(tally(got, pencils), "gy")
-    new_fields = finish(got, full)
-    return new_fields.reshape(fields.shape), summarize(last, coeffs)
+    new_fields, summary = finish(last, got, full, ratio)
+    return new_fields.reshape(fields.shape), summary
 
 
 def solution(mesh):

time: 94.2 us -> 90.1 us (0.956)
  blocking collectives: 57 us -> 76.2 us
  starting transfers between devices: 10.8 us -> 0 us
  local copies, waits for them, and re-layouts: 9.37 us -> 2.49 us
  waiting for transfers between devices: 5.7 us -> 0 us
    all_to_all x4 -> x6, blocking collectives: 57 us -> 76.2 us  [swap(): return lax.all_to_all(x, axis, 0, 0, tiled=True)]
    all_to_all x2 -> x0, starting transfers between devices: 10.8 us -> none  [swap(): return lax.all_to_all(x, axis, 0, 0, tiled=True)]
    unnamed x14 -> x4, local copies, waits for them, and re-layouts: 9.36 us -> 2.49 us
    all_to_all x2 -> x0, waiting for transfers between devices: 5.7 us -> none  [swap(): return lax.all_to_all(x, axis, 0, 0, tiled=True)]
    pallas_call x5 -> x4, Pallas kernels: 8.99 us -> 9.84 us  [the longest x1 7.23 us: gram_partial(): pl.pallas_call(gram_kernel, out_shape=(jax.ShapeDtypeStruct((copies, 8, L...]
  transfers between devices with their start and end apart: 2 -> 0, of which waited for: 2 -> 0; matrix products, arithmetic and copies ran while one was open for 0% -> 0% of each run, Pallas kernels for 2% -> 0%
where the time goes in v2:
time: 90.1 us; the launch traced here: 89.7 us
  blocking collectives  76.2 us (85%)
  Pallas kernels  10.3 us (11%)
  local copies, waits for them, and re-layouts  2.49 us (3%)
    all_to_all x6, blocking collectives, swap(): return lax.all_to_all(x, axis, 0, 0, tiled=True)  76.2 us
    pallas_call x1, Pallas kernels, gram_partial(): pl.pallas_call(gram_kernel, out_shape=(jax.ShapeDtypeStruct((copies, 8, L...  7.23 us
    unnamed x4, local copies, waits for them, and re-layouts  2.49 us

profile of v2, /device:TPU:1, one launch (start us, length us, event | category | flops | bytes accessed | tf_op | source)
XLA Modules:
  0.0 89.7 jit_solution(3994507334936966587)
XLA Ops:
  0.6 0.0 copy-start.1
  0.6 7.2 %gram.1 = (f32[32,8,128]{2,1,0:T(8,128)}, f32[512,128]{1,0:T(8,128)S(1)}, f32[20,512,128]{2,1,0:T(8,128)S(1)}) custom-call(f32[512,128]{1,0:T(8,128)} %bitcast.18, f32[512,128]{1,0:T(8,128)} %bitcast.12, f32[20,512,128]{2,1,0:T(8,128)} %bitcast.17), custom_call_target="tpu_custom_call" | custom-call | tf_op jit(solution)/shard_map/gram/pallas_call | solution.py:144
  7.9 21.0 %all_to_all.30.got_ref = f32[32,8,128]{2,1,0:T(8,128)S(1)} all-to-all(f32[32,8,128]{2,1,0:T(8,128)} %get-tuple-element.13), channel_id=1, replica_groups=mesh['gz'=32,'gy'=8] {'gz'}, dimensions={0} | all-to-all | bytes 262144 | tf_op jit(solution)/shard_map/all_to_all | solution.py:451
  28.9 11.0 %all_to_all.31.sums_ref = f32[8,8,128]{2,1,0:T(8,128)S(1)} all-to-all(f32[8,8,128]{2,1,0:T(8,128)S(1)} %relay.1), channel_id=1, replica_groups=mesh['gz'=32,'gy'=8] {'gy'}, dimensions={0} | all-to-all | bytes 65536 | tf_op jit(solution)/shard_map/all_to_all | solution.py:451
  40.0 0.0 copy-done.1
  40.0 0.0 copy-start
  40.0 2.5 %copy-done = f32[20,2,8,32,128]{4,3,2,1,0:T(8,128)S(1)} copy-done((f32[20,2,8,32,128]{4,3,2,1,0:T(8,128)S(1)}, f32[20,2,8,32,128]{4,3,2,1,0:T(8,128)}, u32[]{:S(2)}) %copy-start) | copy-done | bytes 5242904
  42.5 1.8 %mix.1 = (f32[8,4,8,128]{3,2,1,0:T(8,128)S(1)}, f32[8,128]{1,0:T(8,128)S(1)}, f32[512,128]{1,0:T(8,128)S(1)}, f32[5,32,128]{2,1,0:T(8,128)S(1)}) custom-call(f32[8,8,128]{2,1,0:T(8,128)S(1)} %all_to_all.31.sums_ref, f32[512,128]{1,0:T(8,128)S(1)} %get-tuple-element.14.res_ref, f32[20,512,128]{2,1,0:T(8,128)S(1)} %get-tuple-element.15.past_ref, ...), custom_call_target="tpu_custom_call" | custom-call | tf_op jit(solution)/shard_map/mix/pallas_call | solution.py:266
  44.3 8.4 %all_to_all.32.ends_ref = f32[8,4,8,128]{3,2,1,0:T(8,128)S(1)} all-to-all(f32[8,4,8,128]{3,2,1,0:T(8,128)S(1)} %get-tuple-element.16), channel_id=1, replica_groups=mesh['gz'=32,'gy'=8] {'gy'}, dimensions={0} | all-to-all | bytes 262144 | tf_op jit(solution)/shard_map/all_to_all | solution.py:451
  52.6 0.3 column_part.1
  52.9 12.5 %all_to_all.33 = f32[32,8,128]{2,1,0:T(8,128)S(1)} all-to-all(f32[32,8,128]{2,1,0:T(8,128)S(1)} %bitcast.16), channel_id=1, replica_groups=mesh['gz'=32,'gy'=8] {'gz'}, dimensions={0} | all-to-all | bytes 262144 | tf_op jit(solution)/shard_map/all_to_all | solution.py:451
  65.4 0.2 owner_part.1
  65.6 12.7 %all_to_all.34 = f32[32,8,128]{2,1,0:T(8,128)S(1)} all-to-all(f32[32,8,128]{2,1,0:T(8,128)S(1)} %bitcast.15), channel_id=1, replica_groups=mesh['gz'=32,'gy'=8] {'gz'}, dimensions={0} | all-to-all | bytes 262144 | tf_op jit(solution)/shard_map/all_to_all | solution.py:451
  78.3 10.6 %all_to_all.35.last_ref = f32[8,8,128]{2,1,0:T(8,128)S(1)} all-to-all(f32[8,8,128]{2,1,0:T(8,128)S(1)} %tally.1), channel_id=1, replica_groups=mesh['gz'=32,'gy'=8] {'gy'}, dimensions={0} | all-to-all | bytes 65536 | tf_op jit(solution)/shard_map/all_to_all | solution.py:451
  88.9 0.8 finish.1
  (2 shorter events, 0.1 us)
Async XLA Ops:
  0.6 39.4 %copy-start.1 = (f32[2,8,32,128]{3,2,1,0:T(8,128)S(1)}, f32[2,8,32,128]{3,2,1,0:T(8,128)}, u32[]{:S(2)}) copy-start(f32[2,8,32,128]{3,2,1,0:T(8,128)} %param.4) | copy-start | bytes 786436
  40.0 2.5 %copy-start = (f32[20,2,8,32,128]{4,3,2,1,0:T(8,128)S(1)}, f32[20,2,8,32,128]{4,3,2,1,0:T(8,128)}, u32[]{:S(2)}) copy-start(f32[20,2,8,32,128]{4,3,2,1,0:T(8,128)} %param.6) | copy-start | bytes 15728644

commit v3 on v2

--- a/solution.py
+++ b/solution.py
@@ -157,7 +157,7 @@
             pltpu.VMEM((2, BANDS * 8, BANDS * 8), F32),
             pltpu.SemaphoreType.DMA((LINES // CHUNK + 2,)),
         ],
-        compiler_params=params(54),
+        compiler_params=params(4),
         name="gram",
     )(*(pltpu.with_memory_space_constraint(x, pltpu.HBM) for x in (res, fld, past)))
 
@@ -174,6 +174,7 @@
         in_specs=[VMEM],
         out_specs=VMEM,
         compiler_params=params(4),
+        cost_estimate=pl.CostEstimate(flops=5_000_000_000, bytes_accessed=163840, transcendentals=0),
         name="relay",
     )(got)
 

time: 90.1 us -> 87 us (0.966)
  local copies, waits for them, and re-layouts: 2.49 us -> 0.01 us
    unnamed x4 -> x6, local copies, waits for them, and re-layouts: 2.49 us -> 0.01 us
where the time goes in v3:
time: 87 us; the launch traced here: 86.7 us
  blocking collectives  76.4 us (88%)
  Pallas kernels  9.66 us (11%)
    all_to_all x6, blocking collectives, swap(): return lax.all_to_all(x, axis, 0, 0, tiled=True)  76.4 us
    pallas_call x1, Pallas kernels, gram_partial(): pl.pallas_call(gram_kernel, out_shape=(jax.ShapeDtypeStruct((copies, 8, L...  6.54 us
    pallas_call x1, Pallas kernels, mix(): pl.pallas_call(mix_kernel, out_shape=(jax.ShapeDtypeStruct((copies, 4, PL...  1.78 us

profile of v3, /device:TPU:1, one launch (start us, length us, event | category | flops | bytes accessed | tf_op | source)
XLA Modules:
  0.0 86.7 jit_solution(10725027159934748803)
XLA Ops:
  0.6 6.5 %gram.1 = (f32[32,8,128]{2,1,0:T(8,128)S(1)}, f32[512,128]{1,0:T(8,128)S(1)}, f32[20,512,128]{2,1,0:T(8,128)S(1)}) custom-call(f32[512,128]{1,0:T(8,128)} %bitcast.20, f32[512,128]{1,0:T(8,128)} %bitcast.14, f32[20,512,128]{2,1,0:T(8,128)} %bitcast.19), custom_call_target="tpu_custom_call" | custom-call | tf_op jit(solution)/shard_map/gram/pallas_call | solution.py:144
  7.2 0.0 slice-start
  7.2 21.1 %all_to_all.30.got_ref = f32[32,8,128]{2,1,0:T(8,128)S(1)} all-to-all(f32[32,8,128]{2,1,0:T(8,128)S(1)} %get-tuple-element.13), channel_id=1, replica_groups=mesh['gz'=32,'gy'=8] {'gz'}, dimensions={0} | all-to-all | bytes 262144 | tf_op jit(solution)/shard_map/all_to_all | solution.py:452
  28.3 0.0 slice-start.1
  28.3 0.0 copy-start
  28.3 11.2 %all_to_all.31.sums_ref = f32[8,8,128]{2,1,0:T(8,128)S(1)} all-to-all(f32[8,8,128]{2,1,0:T(8,128)S(1)} %relay.1), channel_id=1, replica_groups=mesh['gz'=32,'gy'=8] {'gy'}, dimensions={0} | all-to-all | bytes 65536 | tf_op jit(solution)/shard_map/all_to_all | solution.py:452
  39.5 0.0 slice-done
  39.5 0.0 slice-done.1
  39.5 0.0 copy-done
  39.5 1.8 %mix.1 = (f32[8,4,8,128]{3,2,1,0:T(8,128)S(1)}, f32[8,128]{1,0:T(8,128)S(1)}, f32[512,128]{1,0:T(8,128)S(1)}, f32[5,32,128]{2,1,0:T(8,128)S(1)}) custom-call(f32[8,8,128]{2,1,0:T(8,128)S(1)} %all_to_all.31.sums_ref, f32[512,128]{1,0:T(8,128)S(1)} %get-tuple-element.14.res_ref, f32[20,512,128]{2,1,0:T(8,128)S(1)} %get-tuple-element.15.past_ref, ...), custom_call_target="tpu_custom_call" | custom-call | tf_op jit(solution)/shard_map/mix/pallas_call | solution.py:267
  41.3 8.4 %all_to_all.32.ends_ref = f32[8,4,8,128]{3,2,1,0:T(8,128)S(1)} all-to-all(f32[8,4,8,128]{3,2,1,0:T(8,128)S(1)} %get-tuple-element.16), channel_id=1, replica_groups=mesh['gz'=32,'gy'=8] {'gy'}, dimensions={0} | all-to-all | bytes 262144 | tf_op jit(solution)/shard_map/all_to_all | solution.py:452
  49.7 0.3 column_part.1
  50.0 12.5 %all_to_all.33 = f32[32,8,128]{2,1,0:T(8,128)S(1)} all-to-all(f32[32,8,128]{2,1,0:T(8,128)S(1)} %bitcast.18), channel_id=1, replica_groups=mesh['gz'=32,'gy'=8] {'gz'}, dimensions={0} | all-to-all | bytes 262144 | tf_op jit(solution)/shard_map/all_to_all | solution.py:452
  62.4 0.2 owner_part.1
  62.6 12.7 %all_to_all.34 = f32[32,8,128]{2,1,0:T(8,128)S(1)} all-to-all(f32[32,8,128]{2,1,0:T(8,128)S(1)} %bitcast.17), channel_id=1, replica_groups=mesh['gz'=32,'gy'=8] {'gz'}, dimensions={0} | all-to-all | bytes 262144 | tf_op jit(solution)/shard_map/all_to_all | solution.py:452
  75.3 10.6 %all_to_all.35.last_ref = f32[8,8,128]{2,1,0:T(8,128)S(1)} all-to-all(f32[8,8,128]{2,1,0:T(8,128)S(1)} %tally.1), channel_id=1, replica_groups=mesh['gz'=32,'gy'=8] {'gy'}, dimensions={0} | all-to-all | bytes 65536 | tf_op jit(solution)/shard_map/all_to_all | solution.py:452
  85.9 0.8 finish.1
  (3 shorter events, 0.1 us)
Async XLA Ops:
  7.2 32.3 %slice-start = ((s8[5242880]{0:T(1024)(128)(4,1)}), s8[4194304]{0:T(1024)(128)(4,1)S(1)}, s32[]{:S(2)}) async-start(s8[5242880]{0:T(1024)(128)(4,1)} %bitcast.9), calls=%async_computation.6 | async-start | bytes 8388608
  28.3 11.2 %slice-start.1 = ((s8[5242880]{0:T(1024)(128)(4,1)}), s8[1048576]{0:T(1024)(128)(4,1)S(1)}, s32[]{:S(2)}) async-start(s8[5242880]{0:T(1024)(128)(4,1)} %bitcast.9), calls=%async_computation.7 | async-start | bytes 2097152
  28.3 11.2 %copy-start = (f32[2,8,32,128]{3,2,1,0:T(8,128)S(1)}, f32[2,8,32,128]{3,2,1,0:T(8,128)}, u32[]{:S(2)}) copy-start(f32[2,8,32,128]{3,2,1,0:T(8,128)} %param.4) | copy-start | bytes 786436

commit v4 on v3

--- a/solution.py
+++ b/solution.py
@@ -16,6 +16,7 @@
 BANDS = HIST + 2
 LINES = 512
 CHUNK = 64
+AHEAD = 3
 LANES = 128
 PLANES = 8
 ROWS = 32
@@ -79,70 +80,92 @@
     return jnp.where(col < row, below, jnp.where(col > row, above, 0.0))
 
 
-def gram_kernel(res_any, fld_any, past_any, out_ref, res_ref, past_ref, fld_ref, high_ref, low_ref, acc_ref, sems):
+def thirds(x):
+    high, rest = halves(x)
+    rest = x - high.astype(F32)
+    middle, low = halves(rest)
+    return high, middle, low
+
+
+def select(picker, x, contract):
+    return functools.reduce(jnp.add, (product(picker, part, contract) for part in thirds(x)))
+
+
+def gram_kernel(ahead, res_any, fld_any, past_any, out_ref, res_ref, past_ref, fld_ref, high_ref, low_ref, acc_ref, sems):
     steps = LINES // CHUNK
     copies = [
         pltpu.make_async_copy(res_any, res_ref, sems.at[steps]),
         pltpu.make_async_copy(fld_any, fld_ref, sems.at[steps + 1]),
     ]
-    chunks = []
-    for t in range(steps):
+
+    def chunk(t):
         rows = pl.ds(CHUNK * t, CHUNK)
-        chunks.append(pltpu.make_async_copy(past_any.at[:, rows], past_ref.at[:, rows], sems.at[t]))
-    for copy in copies + chunks:
+        return pltpu.make_async_copy(past_any.at[:, rows], past_ref.at[:, rows], sems.at[t])
+
+    for copy in copies:
         copy.start()
+    for t in range(ahead):
+        chunk(t).start()
+    acc_ref[...] = jnp.zeros_like(acc_ref)
     for copy in copies:
         copy.wait()
 
     def split(t):
+        slot = t & 1
         for k in range(CHUNK // 8):
-            rows = slice(CHUNK * t + 8 * k, CHUNK * t + 8 * k + 8)
+            rows = pl.ds(pl.multiple_of(CHUNK * t + 8 * k, 8), 8)
             res = res_ref[rows, :]
             delta = res[None] - past_ref[:, rows, :]
             band = jnp.concatenate(
                 [delta.reshape(HIST * 8, LANES), res, fld_ref[rows, :]], axis=0
             )
             columns = slice(LANES * k, LANES * k + LANES)
-            high_ref[t % 2, :, columns], low_ref[t % 2, :, columns] = halves(band)
+            high_ref[slot, :, columns], low_ref[slot, :, columns] = halves(band)
 
     def multiply(t):
-        high = high_ref[t % 2]
-        low = low_ref[t % 2]
-        for k, part in enumerate((high, low)):
-            value = product(high, part, ((1,), (1,)))
-            if t == 0:
-                acc_ref[k] = value
-            else:
-                acc_ref[k] += value
-
-    chunks[0].wait()
+        slot = t & 1
+        high = high_ref[slot]
+        acc_ref[0] += product(high, high, ((1,), (1,)))
+        acc_ref[1] += product(high, low_ref[slot], ((1,), (1,)))
+
+    chunk(0).wait()
+    chunk(ahead).start()
     split(0)
-    for t in range(steps):
-        if t + 1 < steps:
-            chunks[t + 1].wait()
-            split(t + 1)
-        multiply(t)
+
+    def step(t, carry):
+        chunk(t).wait()
+
+        @pl.when(t + ahead < steps)
+        def _():
+            chunk(t + ahead).start()
+
+        split(t)
+        multiply(t - 1)
+        return carry
+
+    lax.fori_loop(1, steps, step, 0)
+    multiply(steps - 1)
 
     size = BANDS * 8
     same = (iota((size, size), 0) & 7) == (iota((size, size), 1) & 7)
     major = jnp.where(same, acc_ref[0] + acc_ref[1], 0.0)
     minor = jnp.where(same, acc_ref[1], 0.0)
-    columns = (iota((size, LANES), 0) >> 3 == iota((size, LANES), 1)).astype(F32)
-    rows = (iota((24, size), 1) >> 3 == iota((24, size), 0)).astype(F32)
-    half = lax.dot(rows, major, precision=EXACT) + lax.dot_general(
-        rows, minor, (((1,), (1,)), ((), ())), precision=EXACT
-    )
-    folded = lax.dot(half, columns, precision=EXACT)
+    columns = (iota((size, LANES), 0) >> 3 == iota((size, LANES), 1)).astype(BF16)
+    rows = (iota((24, size), 1) >> 3 == iota((24, size), 0)).astype(BF16)
+    half = select(rows, major, ((1,), (0,))) + select(rows, minor, ((1,), (1,)))
+    folded = functools.reduce(
+        jnp.add, (product(part, columns, ((1,), (0,))) for part in thirds(half))
+    )
     packed = (
         folded[0:8] + pltpu.roll(folded[8:16], 32, 1) + pltpu.roll(folded[16:24], 64, 1)
     )
     out_ref[...] = jnp.broadcast_to(packed[None], out_ref.shape)
 
 
-def gram_partial(res, fld, past, copies):
+def gram_partial(res, fld, past, copies, ahead=AHEAD):
     wide = (CHUNK // 8) * LANES
     return pl.pallas_call(
-        gram_kernel,
+        functools.partial(gram_kernel, ahead),
         out_shape=(
             jax.ShapeDtypeStruct((copies, 8, LANES), F32),
             pltpu.VMEM((LINES, LANES), F32),

time: 87 us -> 86.4 us (level)
  no operation moved by 1% of the time
where the time goes in v4:
time: 86.4 us; the launch traced here: 86.1 us
  blocking collectives  76.4 us (88%)
  Pallas kernels  9.01 us (10%)
    all_to_all x6, blocking collectives, swap(): return lax.all_to_all(x, axis, 0, 0, tiled=True)  76.4 us
    pallas_call x1, Pallas kernels, gram_partial(): pl.pallas_call(functools.partial(gram_kernel, ahead), out_shape=(jax.Shap...  5.89 us
    pallas_call x1, Pallas kernels, mix(): pl.pallas_call(mix_kernel, out_shape=(jax.ShapeDtypeStruct((copies, 4, PL...  1.78 us

profile of v4, /device:TPU:1, one launch (start us, length us, event | category | flops | bytes accessed | tf_op | source)
XLA Modules:
  0.0 86.1 jit_solution(15846417991827350312)
XLA Ops:
  0.6 5.9 %gram.1 = (f32[32,8,128]{2,1,0:T(8,128)S(1)}, f32[512,128]{1,0:T(8,128)S(1)}, f32[20,512,128]{2,1,0:T(8,128)S(1)}) custom-call(f32[512,128]{1,0:T(8,128)} %bitcast.20, f32[512,128]{1,0:T(8,128)} %bitcast.14, f32[20,512,128]{2,1,0:T(8,128)} %bitcast.19), custom_call_target="tpu_custom_call" | custom-call | tf_op jit(solution)/shard_map/gram/pallas_call | solution.py:167
  6.5 0.0 slice-start
  6.5 21.1 %all_to_all.30.got_ref = f32[32,8,128]{2,1,0:T(8,128)S(1)} all-to-all(f32[32,8,128]{2,1,0:T(8,128)S(1)} %get-tuple-element.13), channel_id=1, replica_groups=mesh['gz'=32,'gy'=8] {'gz'}, dimensions={0} | all-to-all | bytes 262144 | tf_op jit(solution)/shard_map/all_to_all | solution.py:475
  27.6 0.0 slice-start.1
  27.6 0.0 copy-start
  27.7 11.2 %all_to_all.31.sums_ref = f32[8,8,128]{2,1,0:T(8,128)S(1)} all-to-all(f32[8,8,128]{2,1,0:T(8,128)S(1)} %relay.1), channel_id=1, replica_groups=mesh['gz'=32,'gy'=8] {'gy'}, dimensions={0} | all-to-all | bytes 65536 | tf_op jit(solution)/shard_map/all_to_all | solution.py:475
  38.8 0.0 slice-done
  38.8 0.0 slice-done.1
  38.8 0.0 copy-done
  38.9 1.8 %mix.1 = (f32[8,4,8,128]{3,2,1,0:T(8,128)S(1)}, f32[8,128]{1,0:T(8,128)S(1)}, f32[512,128]{1,0:T(8,128)S(1)}, f32[5,32,128]{2,1,0:T(8,128)S(1)}) custom-call(f32[8,8,128]{2,1,0:T(8,128)S(1)} %all_to_all.31.sums_ref, f32[512,128]{1,0:T(8,128)S(1)} %get-tuple-element.14.res_ref, f32[20,512,128]{2,1,0:T(8,128)S(1)} %get-tuple-element.15.past_ref, ...), custom_call_target="tpu_custom_call" | custom-call | tf_op jit(solution)/shard_map/mix/pallas_call | solution.py:290
  40.6 8.4 %all_to_all.32.ends_ref = f32[8,4,8,128]{3,2,1,0:T(8,128)S(1)} all-to-all(f32[8,4,8,128]{3,2,1,0:T(8,128)S(1)} %get-tuple-element.16), channel_id=1, replica_groups=mesh['gz'=32,'gy'=8] {'gy'}, dimensions={0} | all-to-all | bytes 262144 | tf_op jit(solution)/shard_map/all_to_all | solution.py:475
  49.0 0.3 column_part.1
  49.3 12.5 %all_to_all.33 = f32[32,8,128]{2,1,0:T(8,128)S(1)} all-to-all(f32[32,8,128]{2,1,0:T(8,128)S(1)} %bitcast.18), channel_id=1, replica_groups=mesh['gz'=32,'gy'=8] {'gz'}, dimensions={0} | all-to-all | bytes 262144 | tf_op jit(solution)/shard_map/all_to_all | solution.py:475
  61.8 0.2 owner_part.1
  62.0 12.7 %all_to_all.34 = f32[32,8,128]{2,1,0:T(8,128)S(1)} all-to-all(f32[32,8,128]{2,1,0:T(8,128)S(1)} %bitcast.17), channel_id=1, replica_groups=mesh['gz'=32,'gy'=8] {'gz'}, dimensions={0} | all-to-all | bytes 262144 | tf_op jit(solution)/shard_map/all_to_all | solution.py:475
  74.7 10.6 %all_to_all.35.last_ref = f32[8,8,128]{2,1,0:T(8,128)S(1)} all-to-all(f32[8,8,128]{2,1,0:T(8,128)S(1)} %tally.1), channel_id=1, replica_groups=mesh['gz'=32,'gy'=8] {'gy'}, dimensions={0} | all-to-all | bytes 65536 | tf_op jit(solution)/shard_map/all_to_all | solution.py:475
  85.3 0.8 finish.1
  (3 shorter events, 0.1 us)
Async XLA Ops:
  6.5 32.3 %slice-start = ((s8[5242880]{0:T(1024)(128)(4,1)}), s8[4194304]{0:T(1024)(128)(4,1)S(1)}, s32[]{:S(2)}) async-start(s8[5242880]{0:T(1024)(128)(4,1)} %bitcast.9), calls=%async_computation.6 | async-start | bytes 8388608
  27.6 11.2 %slice-start.1 = ((s8[5242880]{0:T(1024)(128)(4,1)}), s8[1048576]{0:T(1024)(128)(4,1)S(1)}, s32[]{:S(2)}) async-start(s8[5242880]{0:T(1024)(128)(4,1)} %bitcast.9), calls=%async_computation.7 | async-start | bytes 2097152
  27.6 11.2 %copy-start = (f32[2,8,32,128]{3,2,1,0:T(8,128)S(1)}, f32[2,8,32,128]{3,2,1,0:T(8,128)}, u32[]{:S(2)}) copy-start(f32[2,8,32,128]{3,2,1,0:T(8,128)} %param.4) | copy-start | bytes 786436

commit v5 on v3

--- a/solution.py
+++ b/solution.py
@@ -16,6 +16,7 @@
 BANDS = HIST + 2
 LINES = 512
 CHUNK = 64
+GROUPS = (8,)
 LANES = 128
 PLANES = 8
 ROWS = 32
@@ -79,7 +80,18 @@
     return jnp.where(col < row, below, jnp.where(col > row, above, 0.0))
 
 
-def gram_kernel(res_any, fld_any, past_any, out_ref, res_ref, past_ref, fld_ref, high_ref, low_ref, acc_ref, sems):
+def thirds(x):
+    high, rest = halves(x)
+    rest = x - high.astype(F32)
+    middle, low = halves(rest)
+    return high, middle, low
+
+
+def select(picker, x, contract):
+    return functools.reduce(jnp.add, (product(picker, part, contract) for part in thirds(x)))
+
+
+def gram_kernel(groups, res_any, fld_any, past_any, out_ref, res_ref, past_ref, fld_ref, high_ref, low_ref, acc_ref, sems):
     steps = LINES // CHUNK
     copies = [
         pltpu.make_async_copy(res_any, res_ref, sems.at[steps]),
@@ -96,53 +108,54 @@
 
     def split(t):
         for k in range(CHUNK // 8):
-            rows = slice(CHUNK * t + 8 * k, CHUNK * t + 8 * k + 8)
+            place = CHUNK * t + 8 * k
+            rows = slice(place, place + 8)
             res = res_ref[rows, :]
             delta = res[None] - past_ref[:, rows, :]
             band = jnp.concatenate(
                 [delta.reshape(HIST * 8, LANES), res, fld_ref[rows, :]], axis=0
             )
-            columns = slice(LANES * k, LANES * k + LANES)
-            high_ref[t % 2, :, columns], low_ref[t % 2, :, columns] = halves(band)
-
-    def multiply(t):
-        high = high_ref[t % 2]
-        low = low_ref[t % 2]
-        for k, part in enumerate((high, low)):
+            columns = slice(LANES // 8 * place, LANES // 8 * place + LANES)
+            high_ref[:, columns], low_ref[:, columns] = halves(band)
+
+    def multiply(first, last):
+        columns = slice(LANES // 8 * CHUNK * first, LANES // 8 * CHUNK * last)
+        high = high_ref[:, columns]
+        for k, part in enumerate((high, low_ref[:, columns])):
             value = product(high, part, ((1,), (1,)))
-            if t == 0:
+            if first == 0:
                 acc_ref[k] = value
             else:
                 acc_ref[k] += value
 
-    chunks[0].wait()
-    split(0)
+    done = 0
     for t in range(steps):
-        if t + 1 < steps:
-            chunks[t + 1].wait()
-            split(t + 1)
-        multiply(t)
+        chunks[t].wait()
+        split(t)
+        if t + 1 in groups:
+            multiply(done, t + 1)
+            done = t + 1
 
     size = BANDS * 8
     same = (iota((size, size), 0) & 7) == (iota((size, size), 1) & 7)
     major = jnp.where(same, acc_ref[0] + acc_ref[1], 0.0)
     minor = jnp.where(same, acc_ref[1], 0.0)
-    columns = (iota((size, LANES), 0) >> 3 == iota((size, LANES), 1)).astype(F32)
-    rows = (iota((24, size), 1) >> 3 == iota((24, size), 0)).astype(F32)
-    half = lax.dot(rows, major, precision=EXACT) + lax.dot_general(
-        rows, minor, (((1,), (1,)), ((), ())), precision=EXACT
-    )
-    folded = lax.dot(half, columns, precision=EXACT)
+    columns = (iota((size, LANES), 0) >> 3 == iota((size, LANES), 1)).astype(BF16)
+    rows = (iota((24, size), 1) >> 3 == iota((24, size), 0)).astype(BF16)
+    half = select(rows, major, ((1,), (0,))) + select(rows, minor, ((1,), (1,)))
+    folded = functools.reduce(
+        jnp.add, (product(part, columns, ((1,), (0,))) for part in thirds(half))
+    )
     packed = (
         folded[0:8] + pltpu.roll(folded[8:16], 32, 1) + pltpu.roll(folded[16:24], 64, 1)
     )
     out_ref[...] = jnp.broadcast_to(packed[None], out_ref.shape)
 
 
-def gram_partial(res, fld, past, copies):
-    wide = (CHUNK // 8) * LANES
-    return pl.pallas_call(
-        gram_kernel,
+def gram_partial(res, fld, past, copies, groups=GROUPS):
+    wide = (LINES // 8) * LANES
+    return pl.pallas_call(
+        functools.partial(gram_kernel, groups),
         out_shape=(
             jax.ShapeDtypeStruct((copies, 8, LANES), F32),
             pltpu.VMEM((LINES, LANES), F32),
@@ -152,12 +165,12 @@
         out_specs=(VMEM,) * 3,
         scratch_shapes=[
             pltpu.VMEM((LINES, LANES), F32),
-            pltpu.VMEM((2, BANDS * 8, wide), BF16),
-            pltpu.VMEM((2, BANDS * 8, wide), BF16),
+            pltpu.VMEM((BANDS * 8, wide), BF16),
+            pltpu.VMEM((BANDS * 8, wide), BF16),
             pltpu.VMEM((2, BANDS * 8, BANDS * 8), F32),
             pltpu.SemaphoreType.DMA((LINES // CHUNK + 2,)),
         ],
-        compiler_params=params(4),
+        compiler_params=params(8),
         name="gram",
     )(*(pltpu.with_memory_space_constraint(x, pltpu.HBM) for x in (res, fld, past)))
 

time: 87 us -> 85.5 us (0.983)
  Pallas kernels: 9.66 us -> 8.15 us
    pallas_call x1, Pallas kernels: 6.54 us -> 5.03 us  [gram_partial(): pl.pallas_call(functools.partial(gram_kernel, groups), out_shape=(jax.Sha...]
where the time goes in v5:
time: 85.5 us; the launch traced here: 85.2 us
  blocking collectives  76.4 us (89%)
  Pallas kernels  8.15 us (10%)
    all_to_all x6, blocking collectives, swap(): return lax.all_to_all(x, axis, 0, 0, tiled=True)  76.4 us
    pallas_call x1, Pallas kernels, gram_partial(): pl.pallas_call(functools.partial(gram_kernel, groups), out_shape=(jax.Sha...  5.03 us
    pallas_call x1, Pallas kernels, mix(): pl.pallas_call(mix_kernel, out_shape=(jax.ShapeDtypeStruct((copies, 4, PL...  1.78 us

profile of v5, /device:TPU:1, one launch (start us, length us, event | category | flops | bytes accessed | tf_op | source)
XLA Modules:
  0.0 85.2 jit_solution(13978549571419872513)
XLA Ops:
  0.6 5.0 %gram.1 = (f32[32,8,128]{2,1,0:T(8,128)S(1)}, f32[512,128]{1,0:T(8,128)S(1)}, f32[20,512,128]{2,1,0:T(8,128)S(1)}) custom-call(f32[512,128]{1,0:T(8,128)} %bitcast.20, f32[512,128]{1,0:T(8,128)} %bitcast.14, f32[20,512,128]{2,1,0:T(8,128)} %bitcast.19), custom_call_target="tpu_custom_call" | custom-call | tf_op jit(solution)/shard_map/gram/pallas_call | solution.py:157
  5.7 0.0 slice-start
  5.7 21.1 %all_to_all.30.got_ref = f32[32,8,128]{2,1,0:T(8,128)S(1)} all-to-all(f32[32,8,128]{2,1,0:T(8,128)S(1)} %get-tuple-element.13), channel_id=1, replica_groups=mesh['gz'=32,'gy'=8] {'gz'}, dimensions={0} | all-to-all | bytes 262144 | tf_op jit(solution)/shard_map/all_to_all | solution.py:465
  26.8 0.0 slice-start.1
  26.8 0.0 copy-start
  26.8 11.2 %all_to_all.31.sums_ref = f32[8,8,128]{2,1,0:T(8,128)S(1)} all-to-all(f32[8,8,128]{2,1,0:T(8,128)S(1)} %relay.1), channel_id=1, replica_groups=mesh['gz'=32,'gy'=8] {'gy'}, dimensions={0} | all-to-all | bytes 65536 | tf_op jit(solution)/shard_map/all_to_all | solution.py:465
  38.0 0.0 slice-done
  38.0 0.0 slice-done.1
  38.0 0.0 copy-done
  38.0 1.8 %mix.1 = (f32[8,4,8,128]{3,2,1,0:T(8,128)S(1)}, f32[8,128]{1,0:T(8,128)S(1)}, f32[512,128]{1,0:T(8,128)S(1)}, f32[5,32,128]{2,1,0:T(8,128)S(1)}) custom-call(f32[8,8,128]{2,1,0:T(8,128)S(1)} %all_to_all.31.sums_ref, f32[512,128]{1,0:T(8,128)S(1)} %get-tuple-element.14.res_ref, f32[20,512,128]{2,1,0:T(8,128)S(1)} %get-tuple-element.15.past_ref, ...), custom_call_target="tpu_custom_call" | custom-call | tf_op jit(solution)/shard_map/mix/pallas_call | solution.py:280
  39.8 8.4 %all_to_all.32.ends_ref = f32[8,4,8,128]{3,2,1,0:T(8,128)S(1)} all-to-all(f32[8,4,8,128]{3,2,1,0:T(8,128)S(1)} %get-tuple-element.16), channel_id=1, replica_groups=mesh['gz'=32,'gy'=8] {'gy'}, dimensions={0} | all-to-all | bytes 262144 | tf_op jit(solution)/shard_map/all_to_all | solution.py:465
  48.1 0.3 column_part.1
  48.4 12.5 %all_to_all.33 = f32[32,8,128]{2,1,0:T(8,128)S(1)} all-to-all(f32[32,8,128]{2,1,0:T(8,128)S(1)} %bitcast.18), channel_id=1, replica_groups=mesh['gz'=32,'gy'=8] {'gz'}, dimensions={0} | all-to-all | bytes 262144 | tf_op jit(solution)/shard_map/all_to_all | solution.py:465
  60.9 0.2 owner_part.1
  61.1 12.7 %all_to_all.34 = f32[32,8,128]{2,1,0:T(8,128)S(1)} all-to-all(f32[32,8,128]{2,1,0:T(8,128)S(1)} %bitcast.17), channel_id=1, replica_groups=mesh['gz'=32,'gy'=8] {'gz'}, dimensions={0} | all-to-all | bytes 262144 | tf_op jit(solution)/shard_map/all_to_all | solution.py:465
  73.8 10.6 %all_to_all.35.last_ref = f32[8,8,128]{2,1,0:T(8,128)S(1)} all-to-all(f32[8,8,128]{2,1,0:T(8,128)S(1)} %tally.1), channel_id=1, replica_groups=mesh['gz'=32,'gy'=8] {'gy'}, dimensions={0} | all-to-all | bytes 65536 | tf_op jit(solution)/shard_map/all_to_all | solution.py:465
  84.4 0.8 finish.1
  (3 shorter events, 0.1 us)
Async XLA Ops:
  5.7 32.3 %slice-start = ((s8[5242880]{0:T(1024)(128)(4,1)}), s8[4194304]{0:T(1024)(128)(4,1)S(1)}, s32[]{:S(2)}) async-start(s8[5242880]{0:T(1024)(128)(4,1)} %bitcast.9), calls=%async_computation.6 | async-start | bytes 8388608
  26.8 11.2 %slice-start.1 = ((s8[5242880]{0:T(1024)(128)(4,1)}), s8[1048576]{0:T(1024)(128)(4,1)S(1)}, s32[]{:S(2)}) async-start(s8[5242880]{0:T(1024)(128)(4,1)} %bitcast.9), calls=%async_computation.7 | async-start | bytes 2097152
  26.8 11.2 %copy-start = (f32[2,8,32,128]{3,2,1,0:T(8,128)S(1)}, f32[2,8,32,128]{3,2,1,0:T(8,128)}, u32[]{:S(2)}) copy-start(f32[2,8,32,128]{3,2,1,0:T(8,128)} %param.4) | copy-start | bytes 786436

commit v6 on v5

--- a/solution.py
+++ b/solution.py
@@ -63,10 +63,13 @@
     return jnp.exp(iota(shape, dim).astype(F32) * (sign / DECAY))
 
 
-def near_matrix(count):
-    lag = jnp.abs(iota((count, count), 0) - iota((count, count), 1)).astype(F32)
+def near_bands(count):
+    shape = (count, 3 * count)
+    col = iota(shape, 1)
+    lag = jnp.abs(iota(shape, 0) - (col & (count - 1))).astype(F32)
     half = (0.5 * LENGTH - lag) / DECAY
-    return (jnp.exp(half) + jnp.exp(-half)) * (0.5 / TOTAL)
+    high, low = halves((jnp.exp(half) + jnp.exp(-half)) * (0.5 / TOTAL))
+    return jnp.where(col < 2 * count, high.astype(F32), low.astype(F32)).astype(BF16)
 
 
 def near_value(lag):
@@ -85,10 +88,6 @@
     rest = x - high.astype(F32)
     middle, low = halves(rest)
     return high, middle, low
-
-
-def select(picker, x, contract):
-    return functools.reduce(jnp.add, (product(picker, part, contract) for part in thirds(x)))
 
 
 def gram_kernel(groups, res_any, fld_any, past_any, out_ref, res_ref, past_ref, fld_ref, high_ref, low_ref, acc_ref, sems):
@@ -141,11 +140,14 @@
     major = jnp.where(same, acc_ref[0] + acc_ref[1], 0.0)
     minor = jnp.where(same, acc_ref[1], 0.0)
     columns = (iota((size, LANES), 0) >> 3 == iota((size, LANES), 1)).astype(BF16)
-    rows = (iota((24, size), 1) >> 3 == iota((24, size), 0)).astype(BF16)
-    half = select(rows, major, ((1,), (0,))) + select(rows, minor, ((1,), (1,)))
-    folded = functools.reduce(
-        jnp.add, (product(part, columns, ((1,), (0,))) for part in thirds(half))
-    )
+    rows = (iota((24, size), 1) >> 3 == iota((24, size), 0)).astype(F32)
+    stacked = jnp.concatenate(thirds(major), axis=0)
+    half = product(jnp.concatenate([rows] * 3, axis=1).astype(BF16), stacked, ((1,), (0,)))
+    for part in halves(minor):
+        half = half + product(rows.astype(BF16), part, ((1,), (1,)))
+    parts = [part.astype(F32) for part in thirds(half)]
+    folded = product(jnp.concatenate(parts, axis=0).astype(BF16), columns, ((1,), (0,)))
+    folded = folded[0:24] + folded[24:48] + folded[48:72]
     packed = (
         folded[0:8] + pltpu.roll(folded[8:16], 32, 1) + pltpu.roll(folded[16:24], 64, 1)
     )
@@ -253,7 +255,11 @@
         end_ref[k] = end_ref[0]
     moment_ref[4] = peak
 
-    near_ref[...] = split_product(near_matrix(ROWS), mixed_ref[...], ((1,), (0,)))
+    bands = near_bands(ROWS)
+    for s in range(2):
+        lanes = slice(LANES * PLANES * s, LANES * PLANES * (s + 1))
+        high, low = halves(mixed_ref[:, lanes])
+        near_ref[:, lanes] = product(bands, jnp.concatenate([high, low, high], axis=0), ((1,), (0,)))
     for s in range(2):
         near = lambda z: near_ref[:, LANES * (PLANES * s + z) : LANES * (PLANES * s + z + 1)]
         planes = [near(z) for z in range(PLANES)]

time: 85.5 us -> 85.4 us (level)
  no operation moved by 1% of the time
where the time goes in v6:
time: 85.4 us; the launch traced here: 85.1 us
  blocking collectives  76.4 us (89%)
  Pallas kernels  7.97 us (9%)
    all_to_all x6, blocking collectives, swap(): return lax.all_to_all(x, axis, 0, 0, tiled=True)  76.4 us
    pallas_call x1, Pallas kernels, gram_partial(): pl.pallas_call(functools.partial(gram_kernel, groups), out_shape=(jax.Sha...  4.95 us

profile of v6, /device:TPU:1, one launch (start us, length us, event | category | flops | bytes accessed | tf_op | source)
XLA Modules:
  0.0 85.1 jit_solution(1581782929266922891)
XLA Ops:
  0.6 5.0 %gram.1 = (f32[32,8,128]{2,1,0:T(8,128)S(1)}, f32[512,128]{1,0:T(8,128)S(1)}, f32[20,512,128]{2,1,0:T(8,128)S(1)}) custom-call(f32[512,128]{1,0:T(8,128)} %bitcast.20, f32[512,128]{1,0:T(8,128)} %bitcast.14, f32[20,512,128]{2,1,0:T(8,128)} %bitcast.19), custom_call_target="tpu_custom_call" | custom-call | tf_op jit(solution)/shard_map/gram/pallas_call | solution.py:159
  5.6 0.0 slice-start
  5.6 21.1 %all_to_all.30.got_ref = f32[32,8,128]{2,1,0:T(8,128)S(1)} all-to-all(f32[32,8,128]{2,1,0:T(8,128)S(1)} %get-tuple-element.13), channel_id=1, replica_groups=mesh['gz'=32,'gy'=8] {'gz'}, dimensions={0} | all-to-all | bytes 262144 | tf_op jit(solution)/shard_map/all_to_all | solution.py:471
  26.7 0.0 slice-start.1
  26.7 0.0 copy-start
  26.7 11.2 %all_to_all.31.sums_ref = f32[8,8,128]{2,1,0:T(8,128)S(1)} all-to-all(f32[8,8,128]{2,1,0:T(8,128)S(1)} %relay.1), channel_id=1, replica_groups=mesh['gz'=32,'gy'=8] {'gy'}, dimensions={0} | all-to-all | bytes 65536 | tf_op jit(solution)/shard_map/all_to_all | solution.py:471
  37.9 0.0 slice-done
  37.9 0.0 slice-done.1
  37.9 0.0 copy-done
  37.9 1.7 %mix.1 = (f32[8,4,8,128]{3,2,1,0:T(8,128)S(1)}, f32[8,128]{1,0:T(8,128)S(1)}, f32[512,128]{1,0:T(8,128)S(1)}, f32[5,32,128]{2,1,0:T(8,128)S(1)}) custom-call(f32[8,8,128]{2,1,0:T(8,128)S(1)} %all_to_all.31.sums_ref, f32[512,128]{1,0:T(8,128)S(1)} %get-tuple-element.14.res_ref, f32[20,512,128]{2,1,0:T(8,128)S(1)} %get-tuple-element.15.past_ref, ...), custom_call_target="tpu_custom_call" | custom-call | tf_op jit(solution)/shard_map/mix/pallas_call | solution.py:286
  39.6 8.4 %all_to_all.32.ends_ref = f32[8,4,8,128]{3,2,1,0:T(8,128)S(1)} all-to-all(f32[8,4,8,128]{3,2,1,0:T(8,128)S(1)} %get-tuple-element.16), channel_id=1, replica_groups=mesh['gz'=32,'gy'=8] {'gy'}, dimensions={0} | all-to-all | bytes 262144 | tf_op jit(solution)/shard_map/all_to_all | solution.py:471
  48.0 0.3 column_part.1
  48.3 12.5 %all_to_all.33 = f32[32,8,128]{2,1,0:T(8,128)S(1)} all-to-all(f32[32,8,128]{2,1,0:T(8,128)S(1)} %bitcast.18), channel_id=1, replica_groups=mesh['gz'=32,'gy'=8] {'gz'}, dimensions={0} | all-to-all | bytes 262144 | tf_op jit(solution)/shard_map/all_to_all | solution.py:471
  60.7 0.2 owner_part.1
  60.9 12.7 %all_to_all.34 = f32[32,8,128]{2,1,0:T(8,128)S(1)} all-to-all(f32[32,8,128]{2,1,0:T(8,128)S(1)} %bitcast.17), channel_id=1, replica_groups=mesh['gz'=32,'gy'=8] {'gz'}, dimensions={0} | all-to-all | bytes 262144 | tf_op jit(solution)/shard_map/all_to_all | solution.py:471
  73.6 10.6 %all_to_all.35.last_ref = f32[8,8,128]{2,1,0:T(8,128)S(1)} all-to-all(f32[8,8,128]{2,1,0:T(8,128)S(1)} %tally.1), channel_id=1, replica_groups=mesh['gz'=32,'gy'=8] {'gy'}, dimensions={0} | all-to-all | bytes 65536 | tf_op jit(solution)/shard_map/all_to_all | solution.py:471
  84.3 0.8 finish.1
  (3 shorter events, 0.1 us)
Async XLA Ops:
  5.6 32.3 %slice-start = ((s8[5242880]{0:T(1024)(128)(4,1)}), s8[4194304]{0:T(1024)(128)(4,1)S(1)}, s32[]{:S(2)}) async-start(s8[5242880]{0:T(1024)(128)(4,1)} %bitcast.9), calls=%async_computation.6 | async-start | bytes 8388608
  26.7 11.2 %slice-start.1 = ((s8[5242880]{0:T(1024)(128)(4,1)}), s8[1048576]{0:T(1024)(128)(4,1)S(1)}, s32[]{:S(2)}) async-start(s8[5242880]{0:T(1024)(128)(4,1)} %bitcast.9), calls=%async_computation.7 | async-start | bytes 2097152
  26.7 11.2 %copy-start = (f32[2,8,32,128]{3,2,1,0:T(8,128)S(1)}, f32[2,8,32,128]{3,2,1,0:T(8,128)}, u32[]{:S(2)}) copy-start(f32[2,8,32,128]{3,2,1,0:T(8,128)} %param.4) | copy-start | bytes 786436

commit v7 on v6

--- a/solution.py
+++ b/solution.py
@@ -478,8 +478,8 @@
     fld = fields.reshape(LINES, LANES)
     past_res = past_residuals.reshape(HIST, LINES, LANES)
     past_fld = past_fields.reshape(HIST, LINES, LANES)
-    sums, res, past_res = gram_partial(res, fld, past_res, slabs)
-    sums = swap(relay(swap(sums, "gz"), pencils), "gy")
+    sums, res, past_res = gram_partial(res, fld, past_res, pencils)
+    sums = swap(relay(swap(sums, "gy"), slabs), "gz")
     ends, ratio, base, moments = mix(sums, res, past_res, fld, past_fld, pencils)
     ends = swap(ends, "gy")
     full, send = column_part(ends, base, moments, slabs)

time: 85.4 us -> 85.3 us (level)
  no operation moved by 1% of the time
where the time goes in v7:
time: 85.3 us; the launch traced here: 85 us
  blocking collectives  76.1 us (89%)
  Pallas kernels  8.12 us (10%)
    all_to_all x6, blocking collectives, swap(): return lax.all_to_all(x, axis, 0, 0, tiled=True)  76.1 us
    pallas_call x1, Pallas kernels, gram_partial(): pl.pallas_call(functools.partial(gram_kernel, groups), out_shape=(jax.Sha...  5.09 us
    pallas_call x1, Pallas kernels, mix(): pl.pallas_call(mix_kernel, out_shape=(jax.ShapeDtypeStruct((copies, 4, PL...  1.71 us

profile of v7, /device:TPU:1, one launch (start us, length us, event | category | flops | bytes accessed | tf_op | source)
XLA Modules:
  0.0 85.0 jit_solution(18286302216021525160)
XLA Ops:
  0.6 0.0 slice-start
  0.6 5.1 %gram.1 = (f32[8,8,128]{2,1,0:T(8,128)S(1)}, f32[512,128]{1,0:T(8,128)S(1)}, f32[20,512,128]{2,1,0:T(8,128)S(1)}) custom-call(f32[512,128]{1,0:T(8,128)} %bitcast.20, f32[512,128]{1,0:T(8,128)} %bitcast.14, f32[20,512,128]{2,1,0:T(8,128)} %bitcast.19), custom_call_target="tpu_custom_call" | custom-call | tf_op jit(solution)/shard_map/gram/pallas_call | solution.py:159
  5.7 10.5 %all_to_all.30.got_ref = f32[8,8,128]{2,1,0:T(8,128)S(1)} all-to-all(f32[8,8,128]{2,1,0:T(8,128)S(1)} %get-tuple-element.13), channel_id=1, replica_groups=mesh['gz'=32,'gy'=8] {'gy'}, dimensions={0} | all-to-all | bytes 65536 | tf_op jit(solution)/shard_map/all_to_all | solution.py:471
  16.2 0.0 slice-start.1
  16.2 0.0 copy-start
  16.2 20.1 %all_to_all.31.sums_ref = f32[32,8,128]{2,1,0:T(8,128)S(1)} all-to-all(f32[32,8,128]{2,1,0:T(8,128)S(1)} %relay.1), channel_id=1, replica_groups=mesh['gz'=32,'gy'=8] {'gz'}, dimensions={0} | all-to-all | bytes 262144 | tf_op jit(solution)/shard_map/all_to_all | solution.py:471
  36.4 0.0 slice-done
  36.4 0.0 slice-done.1
  36.4 0.0 copy-done
  36.4 1.7 %mix.1 = (f32[8,4,8,128]{3,2,1,0:T(8,128)S(1)}, f32[8,128]{1,0:T(8,128)S(1)}, f32[512,128]{1,0:T(8,128)S(1)}, f32[5,32,128]{2,1,0:T(8,128)S(1)}) custom-call(f32[32,8,128]{2,1,0:T(8,128)S(1)} %all_to_all.31.sums_ref, f32[512,128]{1,0:T(8,128)S(1)} %get-tuple-element.14.res_ref, f32[20,512,128]{2,1,0:T(8,128)S(1)} %get-tuple-element.15.past_ref, ...), custom_call_target="tpu_custom_call" | custom-call | tf_op jit(solution)/shard_map/mix/pallas_call | solution.py:286
  38.1 9.8 %all_to_all.32.ends_ref = f32[8,4,8,128]{3,2,1,0:T(8,128)S(1)} all-to-all(f32[8,4,8,128]{3,2,1,0:T(8,128)S(1)} %get-tuple-element.16), channel_id=1, replica_groups=mesh['gz'=32,'gy'=8] {'gy'}, dimensions={0} | all-to-all | bytes 262144 | tf_op jit(solution)/shard_map/all_to_all | solution.py:471
  47.9 0.3 column_part.1
  48.2 12.5 %all_to_all.33 = f32[32,8,128]{2,1,0:T(8,128)S(1)} all-to-all(f32[32,8,128]{2,1,0:T(8,128)S(1)} %bitcast.18), channel_id=1, replica_groups=mesh['gz'=32,'gy'=8] {'gz'}, dimensions={0} | all-to-all | bytes 262144 | tf_op jit(solution)/shard_map/all_to_all | solution.py:471
  60.6 0.2 owner_part.1
  60.8 12.7 %all_to_all.34 = f32[32,8,128]{2,1,0:T(8,128)S(1)} all-to-all(f32[32,8,128]{2,1,0:T(8,128)S(1)} %bitcast.17), channel_id=1, replica_groups=mesh['gz'=32,'gy'=8] {'gz'}, dimensions={0} | all-to-all | bytes 262144 | tf_op jit(solution)/shard_map/all_to_all | solution.py:471
  73.5 10.6 %all_to_all.35.last_ref = f32[8,8,128]{2,1,0:T(8,128)S(1)} all-to-all(f32[8,8,128]{2,1,0:T(8,128)S(1)} %tally.1), channel_id=1, replica_groups=mesh['gz'=32,'gy'=8] {'gy'}, dimensions={0} | all-to-all | bytes 65536 | tf_op jit(solution)/shard_map/all_to_all | solution.py:471
  84.2 0.8 finish.1
  (3 shorter events, 0.0 us)
Async XLA Ops:
  0.6 35.7 %slice-start = ((s8[5242880]{0:T(1024)(128)(4,1)}), s8[4194304]{0:T(1024)(128)(4,1)S(1)}, s32[]{:S(2)}) async-start(s8[5242880]{0:T(1024)(128)(4,1)} %bitcast.9), calls=%async_computation.6 | async-start | bytes 8388608
  16.2 20.2 %slice-start.1 = ((s8[5242880]{0:T(1024)(128)(4,1)}), s8[1048576]{0:T(1024)(128)(4,1)S(1)}, s32[]{:S(2)}) async-start(s8[5242880]{0:T(1024)(128)(4,1)} %bitcast.9), calls=%async_computation.7 | async-start | bytes 2097152
  16.2 20.2 %copy-start = (f32[2,8,32,128]{3,2,1,0:T(8,128)S(1)}, f32[2,8,32,128]{3,2,1,0:T(8,128)}, u32[]{:S(2)}) copy-start(f32[2,8,32,128]{3,2,1,0:T(8,128)} %param.4) | copy-start | bytes 786436

commit v8 on v7

--- a/solution.py
+++ b/solution.py
@@ -419,52 +419,52 @@
     )(got)
 
 
-def tally_kernel(got_ref, out_ref):
+def tally_kernel(got_ref, full_ref, out_ref, field_ref):
     energy = jnp.sum(got_ref[pl.ds(4, ROWS, stride=8), :], axis=0, keepdims=True)
     peak = jnp.max(got_ref[pl.ds(5, ROWS, stride=8), :], axis=0, keepdims=True)
     value = jnp.where(iota((8, LANES), 0) == 0, energy, peak)
     out_ref[...] = jnp.broadcast_to(value[None], out_ref.shape)
-
-
-def tally(got, copies):
-    return pl.pallas_call(
-        tally_kernel,
-        out_shape=jax.ShapeDtypeStruct((copies, 8, LANES), F32),
-        in_specs=[VMEM],
-        out_specs=VMEM,
-        compiler_params=params(8),
-        name="tally",
-    )(got)
-
-
-def finish_kernel(last_ref, got_ref, full_ref, ratio_ref, out_ref, summary_ref):
     down = [got_ref[pl.ds(s, ROWS, stride=8), :] for s in range(2)]
     up = [got_ref[pl.ds(2 + s, ROWS, stride=8), :] for s in range(2)]
     for s in range(2):
         for z in range(PLANES):
             rows = slice(ROWS * (PLANES * s + z), ROWS * (PLANES * s + z) + ROWS)
-            out_ref[rows, :] = (
+            field_ref[rows, :] = (
                 full_ref[rows, :]
                 + math.exp(-z / DECAY) * down[s]
                 + math.exp(z / DECAY) * up[s]
             )
+
+
+def tally(got, full, copies):
+    return pl.pallas_call(
+        tally_kernel,
+        out_shape=(
+            jax.ShapeDtypeStruct((copies, 8, LANES), F32),
+            pltpu.VMEM((LINES, LANES), F32),
+        ),
+        in_specs=[VMEM] * 2,
+        out_specs=(VMEM,) * 2,
+        compiler_params=params(8),
+        name="tally",
+    )(got, full)
+
+
+def finish_kernel(last_ref, ratio_ref, summary_ref):
     summary_ref[0] = jnp.sum(last_ref[:, 0, :]) * (1.0 / CELLS)
     summary_ref[1] = jnp.max(ratio_ref[...])
     summary_ref[2] = jnp.max(last_ref[:, 1, :])
 
 
-def finish(last, got, full, ratio):
+def finish(last, ratio):
     return pl.pallas_call(
         finish_kernel,
-        out_shape=(
-            jax.ShapeDtypeStruct((LINES, LANES), F32),
-            jax.ShapeDtypeStruct((3,), F32),
-        ),
-        in_specs=[VMEM] * 4,
-        out_specs=(VMEM, pl.BlockSpec(memory_space=pltpu.SMEM)),
+        out_shape=jax.ShapeDtypeStruct((3,), F32),
+        in_specs=[VMEM] * 2,
+        out_specs=pl.BlockSpec(memory_space=pltpu.SMEM),
         compiler_params=params(8),
         name="finish",
-    )(last, got, full, ratio)
+    )(last, ratio)
 
 
 def swap(x, axis):
@@ -486,9 +486,9 @@
     got = swap(send.reshape(slabs, 8, LANES), "gz")
     send = owner_part(got.reshape(slabs * 8, LANES))
     got = swap(send.reshape(slabs, 8, LANES), "gz").reshape(slabs * 8, LANES)
-    last = swap(tally(got, pencils), "gy")
-    new_fields, summary = finish(last, got, full, ratio)
-    return new_fields.reshape(fields.shape), summary
+    totals, new_fields = tally(got, full, pencils)
+    last = swap(totals, "gy")
+    return new_fields.reshape(fields.shape), finish(last, ratio)
 
 
 def solution(mesh):

time: 85.3 us -> 86.7 us (1.016)
  blocking collectives: 76.1 us -> 65.5 us
  starting transfers between devices: 0 us -> 6.78 us
  waiting for transfers between devices: 0 us -> 4.04 us
    all_to_all x6 -> x5, blocking collectives: 76.1 us -> 65.5 us  [swap(): return lax.all_to_all(x, axis, 0, 0, tiled=True)]
    all_to_all x0 -> x1, starting transfers between devices: none -> 6.78 us  [swap(): return lax.all_to_all(x, axis, 0, 0, tiled=True)]
    all_to_all x0 -> x1, waiting for transfers between devices: none -> 4.04 us  [swap(): return lax.all_to_all(x, axis, 0, 0, tiled=True)]
  transfers between devices with their start and end apart: 0 -> 1, of which waited for: 0 -> 1; matrix products, arithmetic and copies ran while one was open for 0% -> 1% of each run, Pallas kernels for 0% -> 0%
where the time goes in v8:
time: 86.7 us; the launch traced here: 86.3 us
  blocking collectives  65.5 us (76%)
  Pallas kernels  8.6 us (10%)
  starting transfers between devices  6.78 us (8%)
  waiting for transfers between devices  4.04 us (5%)
    all_to_all x5, blocking collectives, swap(): return lax.all_to_all(x, axis, 0, 0, tiled=True)  65.5 us
    all_to_all x1, starting transfers between devices, swap(): return lax.all_to_all(x, axis, 0, 0, tiled=True)  6.78 us
    pallas_call x1, Pallas kernels, gram_partial(): pl.pallas_call(functools.partial(gram_kernel, groups), out_shape=(jax.Sha...  5.09 us
    all_to_all x1, waiting for transfers between devices, swap(): return lax.all_to_all(x, axis, 0, 0, tiled=True)  4.04 us
  transfers between devices with their start and end apart: 1, of which 1 were waited for; matrix products, arithmetic and copies ran while one was open for 1% of the time, Pallas kernels for 0%

profile of v8, /device:TPU:1, one launch (start us, length us, event | category | flops | bytes accessed | tf_op | source)
XLA Modules:
  0.0 86.3 jit_solution(14104553623836377032)
XLA Ops:
  0.6 0.0 slice-start
  0.6 5.1 %gram.1 = (f32[8,8,128]{2,1,0:T(8,128)S(1)}, f32[512,128]{1,0:T(8,128)S(1)}, f32[20,512,128]{2,1,0:T(8,128)S(1)}) custom-call(f32[512,128]{1,0:T(8,128)} %bitcast.20, f32[512,128]{1,0:T(8,128)} %bitcast.13, f32[20,512,128]{2,1,0:T(8,128)} %bitcast.19), custom_call_target="tpu_custom_call" | custom-call | tf_op jit(solution)/shard_map/gram/pallas_call | solution.py:159
  5.7 10.5 %all_to_all.30.got_ref = f32[8,8,128]{2,1,0:T(8,128)S(1)} all-to-all(f32[8,8,128]{2,1,0:T(8,128)S(1)} %get-tuple-element.13), channel_id=1, replica_groups=mesh['gz'=32,'gy'=8] {'gy'}, dimensions={0} | all-to-all | bytes 65536 | tf_op jit(solution)/shard_map/all_to_all | solution.py:471
  16.2 0.0 slice-start.1
  16.2 0.0 copy-start
  16.2 20.1 %all_to_all.31.sums_ref = f32[32,8,128]{2,1,0:T(8,128)S(1)} all-to-all(f32[32,8,128]{2,1,0:T(8,128)S(1)} %relay.1), channel_id=1, replica_groups=mesh['gz'=32,'gy'=8] {'gz'}, dimensions={0} | all-to-all | bytes 262144 | tf_op jit(solution)/shard_map/all_to_all | solution.py:471
  36.4 0.0 slice-done
  36.4 0.0 slice-done.1
  36.4 0.0 copy-done
  36.4 1.7 %mix.1 = (f32[8,4,8,128]{3,2,1,0:T(8,128)S(1)}, f32[8,128]{1,0:T(8,128)S(1)}, f32[512,128]{1,0:T(8,128)S(1)}, f32[5,32,128]{2,1,0:T(8,128)S(1)}) custom-call(f32[32,8,128]{2,1,0:T(8,128)S(1)} %all_to_all.31.sums_ref, f32[512,128]{1,0:T(8,128)S(1)} %get-tuple-element.14.res_ref, f32[20,512,128]{2,1,0:T(8,128)S(1)} %get-tuple-element.15.past_ref, ...), custom_call_target="tpu_custom_call" | custom-call | tf_op jit(solution)/shard_map/mix/pallas_call | solution.py:286
  38.1 9.8 %all_to_all.32.ends_ref = f32[8,4,8,128]{3,2,1,0:T(8,128)S(1)} all-to-all(f32[8,4,8,128]{3,2,1,0:T(8,128)S(1)} %get-tuple-element.16), channel_id=1, replica_groups=mesh['gz'=32,'gy'=8] {'gy'}, dimensions={0} | all-to-all | bytes 262144 | tf_op jit(solution)/shard_map/all_to_all | solution.py:471
  47.9 0.3 column_part.1
  48.2 12.5 %all_to_all.33 = f32[32,8,128]{2,1,0:T(8,128)S(1)} all-to-all(f32[32,8,128]{2,1,0:T(8,128)S(1)} %bitcast.18), channel_id=1, replica_groups=mesh['gz'=32,'gy'=8] {'gz'}, dimensions={0} | all-to-all | bytes 262144 | tf_op jit(solution)/shard_map/all_to_all | solution.py:471
  60.6 0.2 owner_part.1
  60.8 12.7 %all_to_all.34 = f32[32,8,128]{2,1,0:T(8,128)S(1)} all-to-all(f32[32,8,128]{2,1,0:T(8,128)S(1)} %bitcast.17), channel_id=1, replica_groups=mesh['gz'=32,'gy'=8] {'gz'}, dimensions={0} | all-to-all | bytes 262144 | tf_op jit(solution)/shard_map/all_to_all | solution.py:471
  73.5 0.7 tally.1
  74.2 6.8 %all-to-all-start.5 = ((f32[8,8,128]{2,1,0:T(8,128)}), f32[8,8,128]{2,1,0:T(8,128)S(1)}, u32[]{:S(2)}, u32[]{:S(2)}) async-start(f32[8,8,128]{2,1,0:T(8,128)} %get-tuple-element.22), calls=%async_computation.5 | async-start | bytes 65536 | tf_op jit(solution)/shard_map/all_to_all | solution.py:471
  80.9 0.7 copy.6
  81.6 4.0 %all-to-all-done.5.last_ref = f32[8,8,128]{2,1,0:T(8,128)S(1)} async-done(((f32[8,8,128]{2,1,0:T(8,128)}), f32[8,8,128]{2,1,0:T(8,128)S(1)}, u32[]{:S(2)}, u32[]{:S(2)}) %all-to-all-start.5) | async-done | bytes 32800 | tf_op jit(solution)/shard_map/all_to_all | solution.py:471
  85.7 0.6 finish.1
  (2 shorter events, 0.0 us)
Async XLA Ops:
  0.6 35.7 %slice-start = ((s8[5242880]{0:T(1024)(128)(4,1)}), s8[4194304]{0:T(1024)(128)(4,1)S(1)}, s32[]{:S(2)}) async-start(s8[5242880]{0:T(1024)(128)(4,1)} %bitcast.10), calls=%async_computation.6 | async-start | bytes 8388608
  16.2 20.2 %slice-start.1 = ((s8[5242880]{0:T(1024)(128)(4,1)}), s8[1048576]{0:T(1024)(128)(4,1)S(1)}, s32[]{:S(2)}) async-start(s8[5242880]{0:T(1024)(128)(4,1)} %bitcast.10), calls=%async_computation.7 | async-start | bytes 2097152
  16.2 20.2 %copy-start = (f32[2,8,32,128]{3,2,1,0:T(8,128)S(1)}, f32[2,8,32,128]{3,2,1,0:T(8,128)}, u32[]{:S(2)}) copy-start(f32[2,8,32,128]{3,2,1,0:T(8,128)} %param.4) | copy-start | bytes 786436
  74.2 11.5 %all-to-all-start.5 = ((f32[8,8,128]{2,1,0:T(8,128)}), f32[8,8,128]{2,1,0:T(8,128)S(1)}, u32[]{:S(2)}, u32[]{:S(2)}) async-start(f32[8,8,128]{2,1,0:T(8,128)} %get-tuple-element.22), calls=%async_computation.5 | async-start | bytes 65536 | tf_op jit(solution)/shard_map/all_to_all | solution.py:471
